TPU v7x, 32 devices: a whole 2x2x4 slice. The times are simulated.
32 devices in a mesh: row: 4 (over y, core), col: 8 (over z, x).
Axes of the slice: x: 2, y: 2, z: 4, core: 2. Of those that a mesh axis runs over, the one named last changes fastest.
Arguments:
- parent_front: float32 [8, 1024, 4, 2048], P(None, 'row', None, 'col'), may hold values from -6 to 6
- generators: bfloat16 [48, 256, 256], P('row'), may hold values from -1.5 to 1.5
- diagonal_blocks: bfloat16 [48, 256, 256], P('row'), may hold values from -6 to 6
- coupling: bfloat16 [2, 256, 256], replicated, may hold values from -0.375 to 0.375
- block_map: int32 [2, 24], replicated, may hold values from 0 to 31, as said below
- valid_rows: int32 [2, 24], replicated, may hold values from 128 to 256
Outputs:
- assembled: float32 [8, 1024, 4, 2048], P(None, 'row', None, 'col')
Inputs may be any that keep to these rules, and one draw needn't show every extreme that they name: `block_map`: for each child c and each s < 2, the child blocks s * 12 to (s + 1) * 12 - 1 map in increasing order to distinct parent blocks of the range s * 16 to (s + 1) * 16 - 1, and the parent blocks s * 16 + m * 4 of that range always receive one.
All inputs are finite; a program needn't handle non-finite values.
Results may differ from a plain program's by a relative error of at most 0.0028.
Values may be sent and summed in bfloat16 or wider, within the bound.
A program may use at most 128 MiB of HBM per device.

v0:
```python
import functools

import jax
import jax.numpy as jnp
from jax import lax
from jax.experimental import pallas as pl
from jax.experimental.pallas import tpu as pltpu
from jax.sharding import PartitionSpec as P

MESH = pl.DeviceIdType.MESH
QUAD = 4
LANES = 128


def exchange_kernel(
    row_count, col_count, row_cap, col_cap,
    gen_hbm, diag_hbm, coupling_hbm, map_hbm, count_hbm, front_hbm,
    rows_out, cols_out, diag_out, front_out,
    gen_ref, diag_ref, coupling_ref, map_ref, count_ref, load_sem, front_sem,
    send_rows, send_pair, rows_raw, cols_raw, diag_raw,
    far_send, far_recv, quad_send, quad_recv, pair_send, pair_recv,
    col_send, col_recv, fwd_send, fwd_recv, diag_send, diag_recv,
):
    groups = row_count // 2
    group_blocks, block, rank = gen_ref.shape
    window = row_cap * row_count
    chunk = row_cap * block // QUAD
    row = lax.axis_index("row")
    col = lax.axis_index("col")
    group = row // 2
    core = row % 2
    quarter = col % QUAD
    pair_row = group * 2 + 1 - core
    diag_row = col % row_count
    quad_cols = (
        col + 1 - 2 * (quarter % 2),
        col + 2 - 4 * (quarter // 2),
        col + 3 - 2 * quarter,
    )

    def lookup(child, source, slot):
        found = jnp.int32(0)
        count = jnp.int32(0)
        target = source * window + slot
        for k in range(group_blocks):
            hit = map_ref[child, source * group_blocks + k] == target
            found = jnp.where(hit, k, found)
            count = jnp.where(hit, count_ref[child, source * group_blocks + k], count)
        return found, count

    def remote(src, dst, send, recv, to_row, to_col):
        return pltpu.make_async_remote_copy(
            src_ref=src, dst_ref=dst, send_sem=send, recv_sem=recv,
            device_id=(to_row, to_col), device_id_type=MESH,
        )

    loads = [
        pltpu.make_async_copy(src, dst, load_sem.at[n])
        for n, (src, dst) in enumerate((
            (map_hbm, map_ref), (count_hbm, count_ref), (gen_hbm, gen_ref),
            (diag_hbm, diag_ref), (coupling_hbm, coupling_ref),
        ))
    ]
    for load in loads:
        load.start()

    barrier = pltpu.get_barrier_semaphore()
    for k in range(1, row_count):
        pl.semaphore_signal(
            barrier, inc=1, device_id=((row + k) % row_count, col), device_id_type=MESH
        )
    for other in quad_cols:
        pl.semaphore_signal(barrier, inc=1, device_id=(row, other), device_id_type=MESH)

    for load in loads:
        load.wait()
    front_load = pltpu.make_async_copy(front_hbm, front_out, front_sem)
    front_load.start()
    start_row = quarter * chunk
    quarter_slot = start_row // block
    quarter_off = pl.multiple_of(start_row % block, chunk)
    for k in range(1, groups):
        dest = (group + k) % groups
        for r in range(2):
            found, _ = lookup(core, group, quarter_slot * row_count + 2 * dest + r)
            send_rows[k - 1, r] = gen_ref[found, pl.ds(quarter_off, chunk), :]
    for t in range(col_cap):
        found, _ = lookup(core, group, t * col_count + col)
        cols_raw[core, group, pl.ds(t * block, block), :] = gen_ref[found]
        diag_raw[core, group, pl.ds(t * block, block), :] = diag_ref[found]

    pl.semaphore_wait(barrier, row_count - 1 + QUAD - 1)

    sends = []

    def far_copy(k, r, child, source, dest_row):
        return remote(
            send_rows.at[k - 1, r], rows_raw.at[child, source, quarter],
            far_send.at[k - 1, r], far_recv.at[k - 1, child], dest_row, col,
        )

    for k in range(1, groups):
        dest = (group + k) % groups
        for r in range(2):
            copy = far_copy(k, r, core, group, 2 * dest + r)
            copy.start()
            sends.append(copy)

    own_cols = cols_raw.at[core, group]
    for k in range(1, groups):
        dest = (group + k) % groups
        copy = remote(own_cols, own_cols, col_send.at[k], col_recv.at[k], 2 * dest + core, col)
        copy.start()
        sends.append(copy)
    copy = remote(own_cols, own_cols, col_send.at[0], col_recv.at[0], pair_row, col)
    copy.start()
    sends.append(copy)

    own_diag = diag_raw.at[core, group]
    diag_away = remote(
        own_diag, own_diag, diag_send, diag_recv.at[core, group], diag_row, col
    )

    @pl.when(row != diag_row)
    def _():
        diag_away.start()

    for m in range(row_cap):
        found, _ = lookup(core, group, m * row_count + pair_row)
        send_pair[pl.ds(m * block, block), :] = gen_ref[found]
    for j in range(QUAD):
        slot, off = j * chunk // block, j * chunk % block
        found, _ = lookup(core, group, slot * row_count + row)
        rows_raw[core, group, j] = gen_ref[found, off:off + chunk, :]
    for j in range(QUAD):
        copy = remote(
            send_pair.at[pl.ds(j * chunk, chunk)], rows_raw.at[core, group, j],
            pair_send.at[j], pair_recv.at[j], pair_row, col,
        )
        copy.start()
        sends.append(copy)

    row_iota = lax.broadcasted_iota(jnp.int32, (block, rank), 0)
    col_iota = lax.broadcasted_iota(jnp.int32, (block, block), 1)

    def finish_rows(child, source, j):
        slot, off = j * chunk // block, j * chunk % block
        _, count = lookup(child, source, slot * row_count + row)
        kept = (row_iota[off:off + chunk] < count).astype(jnp.float32).astype(jnp.bfloat16)
        rows_out[source, j, :, child * rank:(child + 1) * rank] = rows_raw[child, source, j] * kept

    def finish_cols(child, source):
        for t in range(col_cap):
            _, count = lookup(child, source, t * col_count + col)
            kept = (row_iota < count).astype(jnp.float32).astype(jnp.bfloat16)
            masked = cols_raw[child, source, t * block:(t + 1) * block, :] * kept
            cols_out[source, t, child * rank:(child + 1) * rank, :] = lax.dot_general(
                coupling_ref[child], masked, (((0,), (1,)), ((), ())),
                preferred_element_type=jnp.float32,
            ).astype(jnp.bfloat16)

    for k in range(1, groups):
        source = (group + groups - k) % groups
        for child in range(2):
            far_copy(k, 0, child, source, row).wait_recv()
            landed = rows_raw.at[child, source, quarter]
            for j, other in enumerate(quad_cols):
                copy = remote(
                    landed, landed, quad_send.at[k - 1, child, j], quad_recv.at[k - 1, child, j],
                    row, other,
                )
                copy.start()
                sends.append(copy)

    for j in range(QUAD):
        remote(
            send_pair.at[pl.ds(j * chunk, chunk)], rows_raw.at[1 - core, group, j],
            pair_send.at[j], pair_recv.at[j], pair_row, col,
        ).wait_recv()
    for child in range(2):
        for j in range(QUAD):
            finish_rows(child, group, j)
    remote(own_cols, cols_raw.at[1 - core, group], col_send.at[0], col_recv.at[0], pair_row, col).wait_recv()
    for child in range(2):
        finish_cols(child, group)

    for k in range(1, groups):
        source = (group + groups - k) % groups
        landed = cols_raw.at[core, source]
        remote(own_cols, landed, col_send.at[k], col_recv.at[k], pair_row, col).wait_recv()
        copy = remote(landed, landed, fwd_send.at[k - 1], fwd_recv.at[k - 1], pair_row, col)
        copy.start()
        sends.append(copy)
    for k in range(1, groups):
        source = (group + groups - k) % groups
        remote(
            own_cols, cols_raw.at[1 - core, source], fwd_send.at[k - 1], fwd_recv.at[k - 1], pair_row, col
        ).wait_recv()
        for child in range(2):
            finish_cols(child, source)

    @pl.when(row == diag_row)
    def _():
        for source in range(groups):
            for child in range(2):
                @pl.when(2 * source + child != row)
                def _():
                    remote(
                        own_diag, diag_raw.at[child, source], diag_send, diag_recv.at[child, source],
                        pair_row, col,
                    ).wait_recv()
        for source in range(groups):
            for t in range(col_cap):
                total = jnp.zeros((block, block), jnp.float32)
                for child in range(2):
                    _, count = lookup(child, source, t * col_count + col)
                    inside = jnp.maximum(row_iota, col_iota) < count
                    piece = diag_raw[child, source, t * block:(t + 1) * block, :].astype(jnp.float32)
                    total = total + jnp.where(inside, piece, 0.0)
                diag_out[source, t] = total

    @pl.when(row != diag_row)
    def _():
        diag_out[...] = jnp.zeros_like(diag_out)

    for k in range(1, groups):
        source = (group + groups - k) % groups
        for child in range(2):
            for j, other in enumerate(quad_cols):
                landed = rows_raw.at[child, source, other % QUAD]
                remote(
                    landed, landed, quad_send.at[k - 1, child, j], quad_recv.at[k - 1, child, j],
                    row, other,
                ).wait_recv()
        for child in range(2):
            for j in range(QUAD):
                finish_rows(child, source, j)

    front_load.wait()
    for copy in sends:
        copy.wait_send()

    @pl.when(row != diag_row)
    def _():
        diag_away.wait_send()


def add_kernel(
    row_count, col_count, front_ref, rows_ref, cols_ref, diag_ref, out_ref, staged, out_sem
):
    rows_local = rows_ref.shape[0]
    cols_local, _, block = cols_ref.shape
    halves = block // LANES
    per_row = halves * cols_local
    row = lax.axis_index("row")
    col = lax.axis_index("col")

    def write(a):
        return pltpu.make_async_copy(staged.at[a % 2], out_ref.at[a], out_sem.at[a % 2])

    for a in range(rows_local):
        if a >= 2:
            write(a - 2).wait()
        for b in range(cols_local):
            tile = jnp.dot(rows_ref[a], cols_ref[b], preferred_element_type=jnp.float32)
            for h in range(halves):
                spot = pl.ds(h * cols_local + b, block, stride=per_row)
                staged[a % 2, spot, :] = front_ref[a, spot, :] + tile[:, h * LANES:(h + 1) * LANES]
        row_parent = a * row_count + row

        @pl.when(row_parent % col_count == col)
        def _():
            b = row_parent // col_count
            for h in range(halves):
                spot = pl.ds(h * cols_local + b, block, stride=per_row)
                piece = diag_ref[b, :, h * LANES:(h + 1) * LANES]
                staged[a % 2, spot, :] = staged[a % 2, spot, :] + piece

        write(a).start()
    for a in range(rows_local - 2, rows_local):
        write(a).wait()


def shards(parent_front, generators, diagonal_blocks, coupling, block_map, valid_rows):
    row_count = lax.axis_size("row")
    col_count = lax.axis_size("col")
    groups = row_count // 2
    block, rank = generators.shape[1:]
    rows_local = parent_front.shape[0]
    cols_local = parent_front.shape[2]
    row_cap = rows_local // groups
    col_cap = cols_local // groups
    chunk = row_cap * block // QUAD
    vmem = pl.BlockSpec(memory_space=pltpu.VMEM)
    hbm = pl.BlockSpec(memory_space=pltpu.HBM)
    dma = pltpu.SemaphoreType.DMA
    halves = block // LANES
    per_row = halves * cols_local
    flat = parent_front.reshape(rows_local, block, cols_local, halves, LANES)
    flat = flat.transpose(0, 1, 3, 2, 4).reshape(rows_local, block * per_row, LANES)
    operands = [
        pltpu.with_memory_space_constraint(x, pltpu.HBM)
        for x in (generators, diagonal_blocks, coupling, block_map, valid_rows, flat)
    ]
    rows, cols, diag, front = pl.pallas_call(
        functools.partial(exchange_kernel, row_count, col_count, row_cap, col_cap),
        out_shape=(
            pltpu.VMEM((groups, QUAD, chunk, 2 * rank), jnp.bfloat16),
            pltpu.VMEM((groups, col_cap, 2 * rank, block), jnp.bfloat16),
            pltpu.VMEM((groups, col_cap, block, block), jnp.float32),
            pltpu.VMEM(flat.shape, jnp.float32),
        ),
        in_specs=[hbm] * 6,
        out_specs=(vmem,) * 4,
        scratch_shapes=[
            pltpu.VMEM(generators.shape, jnp.bfloat16),
            pltpu.VMEM(diagonal_blocks.shape, jnp.bfloat16),
            pltpu.VMEM(coupling.shape, jnp.bfloat16),
            pltpu.SMEM(block_map.shape, jnp.int32),
            pltpu.SMEM(valid_rows.shape, jnp.int32),
            dma((5,)),
            dma,
            pltpu.VMEM((groups - 1, 2, chunk, rank), jnp.bfloat16),
            pltpu.VMEM((row_cap * block, rank), jnp.bfloat16),
            pltpu.VMEM((2, groups, QUAD, chunk, rank), jnp.bfloat16),
            pltpu.VMEM((2, groups, col_cap * block, rank), jnp.bfloat16),
            pltpu.VMEM((2, groups, col_cap * block, block), jnp.bfloat16),
            dma((groups - 1, 2)),
            dma((groups - 1, 2)),
            dma((groups - 1, 2, QUAD - 1)),
            dma((groups - 1, 2, QUAD - 1)),
            dma((QUAD,)),
            dma((QUAD,)),
            dma((groups,)),
            dma((groups,)),
            dma((groups - 1,)),
            dma((groups - 1,)),
            dma,
            dma((2, groups)),
        ],
        compiler_params=pltpu.CompilerParams(
            collective_id=0, has_side_effects=True, vmem_limit_bytes=32 * 1024 * 1024
        ),
    )(*operands)
    rows = rows.reshape(rows_local, block, 2 * rank)
    cols = cols.reshape(cols_local, 2 * rank, block)
    diag = diag.reshape(cols_local, block, block)
    out = pl.pallas_call(
        functools.partial(add_kernel, row_count, col_count),
        out_shape=jax.ShapeDtypeStruct(flat.shape, jnp.float32),
        in_specs=[vmem] * 4,
        out_specs=hbm,
        scratch_shapes=[pltpu.VMEM((2,) + flat.shape[1:], jnp.float32), dma((2,))],
        compiler_params=pltpu.CompilerParams(vmem_limit_bytes=32 * 1024 * 1024),
    )(*(pltpu.with_memory_space_constraint(x, pltpu.VMEM) for x in (front, rows, cols, diag)))
    out = out.reshape(rows_local, block, halves, cols_local, LANES)
    return out.transpose(0, 1, 3, 2, 4).reshape(parent_front.shape)


def solution(mesh):
    in_specs = (
        P(None, "row", None, "col"),
        P("row", None, None),
        P("row", None, None),
        P(),
        P(),
        P(),
    )
    out_specs = P(None, "row", None, "col")
    return jax.shard_map(shards, mesh=mesh, in_specs=in_specs, out_specs=out_specs, check_vma=False)
```

profile of v0, /device:TPU:1, one launch (start us, length us, event | category | flops | bytes accessed | tf_op | source)
XLA Modules:
  0.0 31.1 jit_solution(4828564964532914909)
XLA Ops:
  0.0 24.5 %shard_map.64 = (bf16[2,4,256,512]{3,2,1,0:T(8,128)(2,1)S(1)}, bf16[2,2,512,256]{3,2,1,0:T(8,128)(2,1)S(1)}, f32[2,2,256,256]{3,2,1,0:T(8,128)S(1)}, f32[8,2048,128]{2,1,0:T(8,128)S(1)}) custom-call(bf16[12,256,256]{2,1,0:T(8,128)(2,1)} %gen_hbm.1, bf16[12,256,256]{2,1,0:T(8,128)(2,1)} %diag_hbm.1, bf16[2,256,256]{2,1,0:T(8,128)(2,1)} %coupling_hbm.1, ...), custom_call_target="tpu_custom_call" | custom-call | tf_op jit(solution)/shard_map/pallas_call | solution.py:305
  24.5 6.6 %shard_map.65 = f32[8,2048,128]{2,1,0:T(8,128)} custom-call(f32[8,2048,128]{2,1,0:T(8,128)S(1)} %get-tuple-element.9.front_ref, bf16[8,256,512]{2,1,0:T(8,128)(2,1)S(1)} %bitcast.13, bf16[4,512,256]{2,1,0:T(8,128)(2,1)S(1)} %bitcast.14, f32[4,256,256]{2,1,0:T(8,128)S(1)} %bitcast.15), custom_call_target="tpu_custom_call" | custom-call | tf_op jit(solution)/shard_map/pallas_call | solution.py:348
where the time goes:
time: 31.3 us; the launch traced here: 31.1 us
  Pallas kernels  31.1 us (99%)
    pallas_call x1, Pallas kernels, shards(): pl.pallas_call(functools.partial(exchange_kernel, row_count, col_count, r...  24.5 us
    pallas_call x1, Pallas kernels, shards(): pl.pallas_call(functools.partial(add_kernel, row_count, col_count), out_s...  6.61 us

commit v1 on v0

v1 whole, which is shorter than its diff:
```python
import functools

import jax
import jax.numpy as jnp
from jax import lax
from jax.experimental import pallas as pl
from jax.experimental.pallas import tpu as pltpu
from jax.sharding import PartitionSpec as P

MESH = pl.DeviceIdType.MESH
QUAD = 4
LANES = 128
PIECES = 2
LAG = 2


def exchange_kernel(
    row_count, col_count, row_cap, col_cap,
    gen_hbm, diag_hbm, coupling_hbm, map_hbm, count_hbm, front_hbm,
    rows_out, cols_out, diag_out, front_out,
    gen_ref, diag_ref, coupling_ref, map_ref, count_ref, load_sem, front_sem,
    far_rows, pair_rows, own_diag,
    far_send, far_recv, x_send, x_recv, z_send, z_recv, xr_send, xr_recv, zr_send, zr_recv,
    pair_send, pair_recv, near_send, near_recv, col_send, col_recv, fwd_send, fwd_recv,
    over_send, over_recv, diag_send, diag_recv,
):
    groups = row_count // 2
    group_blocks, block, rank = gen_ref.shape
    window = row_cap * row_count
    rows_of = block // PIECES
    steps = [(t, p) for t in range(col_cap) for p in range(PIECES)]
    row = lax.axis_index("row")
    col = lax.axis_index("col")
    group = row // 2
    core = row % 2
    quarter = col % QUAD
    half = col // row_count
    pair_row = group * 2 + 1 - core
    diag_row = col % row_count
    x_col = col + 1 - 2 * (quarter % 2)
    z_col = col + 2 - 4 * (quarter // 2)
    holder = quarter % 2 == core

    def parity(dest):
        return jnp.where(quarter // 2 == dest % 2, half, 1 - half)

    def overlaps(dest):
        return diag_row // 2 == dest

    def lookup(child, source, slot):
        found = jnp.int32(0)
        count = jnp.int32(0)
        target = source * window + slot
        for d in range(window - group_blocks + 1):
            k = jnp.clip(slot - d, 0, group_blocks - 1)
            hit = map_ref[child, source * group_blocks + k] == target
            found = jnp.where(hit, k, found)
            count = jnp.where(hit, count_ref[child, source * group_blocks + k], count)
        return found, count

    row_iota = lax.broadcasted_iota(jnp.int32, (block, LANES), 0)

    def masked_rows(slot):
        found, count = lookup(core, group, slot)
        kept = (row_iota < count).astype(jnp.float32).astype(jnp.bfloat16)
        return gen_ref[found] * jnp.concatenate([kept] * (rank // LANES), axis=1)

    def project(child, rows):
        return lax.dot_general(
            coupling_ref[child], rows, (((0,), (1,)), ((), ())),
            preferred_element_type=jnp.float32,
        ).astype(jnp.bfloat16)

    def remote(src, dst, send, recv, to_row, to_col):
        return pltpu.make_async_remote_copy(
            src_ref=src, dst_ref=dst, send_sem=send, recv_sem=recv,
            device_id=(to_row, to_col), device_id_type=MESH,
        )

    def load(src, dst, n):
        return pltpu.make_async_copy(src, dst, load_sem.at[n])

    loads = [
        load(src, dst, n)
        for n, (src, dst) in enumerate((
            (map_hbm, map_ref), (count_hbm, count_ref), (gen_hbm, gen_ref),
            (coupling_hbm, coupling_ref), (diag_hbm, diag_ref),
        ))
    ]
    for copy in loads:
        copy.start()

    barrier = pltpu.get_barrier_semaphore()
    for k in range(1, row_count):
        pl.semaphore_signal(
            barrier, inc=1, device_id=((row + k) % row_count, col), device_id_type=MESH
        )
    for other in (x_col, z_col):
        pl.semaphore_signal(barrier, inc=1, device_id=(row, other), device_id_type=MESH)

    def far_copy(k, child, source, par, t, p, dest_row):
        part = pl.ds(p * rows_of, rows_of)
        return remote(
            far_rows.at[k - 1, t, part], rows_out.at[source, 2 * t + par, child, part],
            far_send.at[k - 1, t, p], far_recv.at[k - 1, child, t, p], dest_row, col,
        )

    def landed(source, par, child, t, p):
        return rows_out.at[source, 2 * t + par, child, pl.ds(p * rows_of, rows_of)]

    def x_copy(k, source, par, child, t, p):
        piece = landed(source, par, child, t, p)
        at = (k - 1, child, t, p)
        return remote(piece, piece, x_send.at[at], x_recv.at[at], row, x_col)

    def z_copy(k, source, par, child, t, p):
        piece = landed(source, par, child, t, p)
        at = (k - 1, child, t, p)
        return remote(piece, piece, z_send.at[at], z_recv.at[at], row, z_col)

    def xr_copy(k, source, par, t, p):
        piece = landed(source, par, 0, t, p)
        at = (k - 1, t, p)
        return remote(piece, piece, xr_send.at[at], xr_recv.at[at], row, x_col)

    def zr_copy(k, source, par, t, p):
        piece = landed(source, par, 1, t, p)
        at = (k - 1, t, p)
        return remote(piece, piece, zr_send.at[at], zr_recv.at[at], row, z_col)

    def pair_copy(child, m):
        return remote(
            pair_rows.at[m], rows_out.at[group, m, child],
            pair_send.at[m], pair_recv.at[m], pair_row, col,
        )

    def near_copy(child, t):
        piece = cols_out.at[group, t, child]
        return remote(piece, piece, near_send.at[t], near_recv.at[t], pair_row, col)

    def col_copy(k, source, t, dest):
        piece = cols_out.at[source, t, core]
        return remote(
            piece, piece, col_send.at[k - 1, t], col_recv.at[k - 1, t], 2 * dest + core, col
        )

    def fwd_copy(k, source, child, t):
        piece = cols_out.at[source, t, child]
        return remote(piece, piece, fwd_send.at[k - 1, t], fwd_recv.at[k - 1, t], pair_row, col)

    def over_copy(k, source, child, t):
        piece = cols_out.at[source, t, child]
        at = (k - 1, child, t)
        return remote(piece, piece, over_send.at[at], over_recv.at[at], pair_row, col)

    def diag_copy(source, child, t):
        return remote(
            own_diag.at[t], diag_out.at[source, child, t],
            diag_send.at[t], diag_recv.at[source, child, t], diag_row, col,
        )

    far = [(k, (group + k) % groups) for k in range(1, groups)]
    sources = [(k, (group + groups - k) % groups) for k in range(1, groups)]
    par = parity(group)

    for copy in loads[:3]:
        copy.wait()
    for t in range(col_cap):
        for k, dest in far:
            slot = (2 * t + parity(dest)) * row_count + 2 * dest + quarter % 2
            far_rows[k - 1, t] = masked_rows(slot)
        if t == 0:
            pl.semaphore_wait(barrier, row_count + 1)
        for k, dest in far:
            for p in range(PIECES):
                far_copy(k, core, group, parity(dest), t, p, 2 * dest + quarter % 2).start()

    front_loads = [
        pltpu.make_async_copy(front_hbm.at[a, :, h], front_out.at[a, h], front_sem.at[a, h])
        for a in range(front_out.shape[0]) for h in range(front_out.shape[1])
    ]
    for copy in loads[3:]:
        copy.wait()

    for t in range(col_cap):
        cols_out[group, t, core] = project(core, masked_rows(t * col_count + col))
        near_copy(core, t).start()
        for k, dest in far:
            @pl.when(jnp.logical_not(overlaps(dest)))
            def _():
                col_copy(k, group, t, dest).start()

    row_iota2 = lax.broadcasted_iota(jnp.int32, (block, block), 0)
    col_iota2 = lax.broadcasted_iota(jnp.int32, (block, block), 1)
    edge = jnp.maximum(row_iota2, col_iota2)
    for t in range(col_cap):
        found, count = lookup(core, group, t * col_count + col)
        piece = jnp.where(edge < count, diag_ref[found].astype(jnp.float32), 0.0)
        own_diag[t] = piece.astype(jnp.bfloat16)

        @pl.when(row != diag_row)
        def _():
            diag_copy(group, core, t).start()

        @pl.when(row == diag_row)
        def _():
            diag_out[group, core, t] = own_diag[t]

    for copy in front_loads:
        copy.start()
    for m in range(row_cap):
        pair_rows[m] = masked_rows(m * row_count + pair_row)
        pair_copy(core, m).start()
    for m in range(row_cap):
        rows_out[group, m, core] = masked_rows(m * row_count + row)

    @pl.when(holder)
    def _():
        for i in range(len(steps) + LAG):
            if i < len(steps):
                t, p = steps[i]
                for k, source in sources:
                    for child in range(2):
                        far_copy(k, child, source, par, t, p, row).wait_recv()
                        x_copy(k, source, par, child, t, p).start()
                        z_copy(k, source, par, child, t, p).start()
            if i >= LAG:
                t, p = steps[i - LAG]
                for k, source in sources:
                    z_copy(k, source, 1 - par, 0, t, p).wait_recv()
                    xr_copy(k, source, 1 - par, t, p).start()
            if i == len(steps) - 1:
                @pl.when(overlaps(group))
                def _():
                    for k, source in sources:
                        for t in range(col_cap):
                            for child in range(2):
                                cols_out[source, t, child] = project(
                                    child, rows_out[source, 2 * t + par, child]
                                )
                                over_copy(k, source, child, t).start()

    @pl.when(jnp.logical_not(holder))
    def _():
        for t, p in steps:
            for k, source in sources:
                x_copy(k, source, par, 1, t, p).wait_recv()
                zr_copy(k, source, par, t, p).start()
                x_copy(k, source, par, 0, t, p).wait_recv()

    @pl.when(jnp.logical_not(overlaps(group)))
    def _():
        for t in range(col_cap):
            for k, source in sources:
                col_copy(k, source, t, group).wait_recv()
                fwd_copy(k, source, core, t).start()

    for copy in front_loads:
        copy.wait()
    for m in range(row_cap):
        pair_copy(1 - core, m).wait_recv()
        pair_copy(core, m).wait_send()
    for t in range(col_cap):
        near_copy(1 - core, t).wait_recv()
        near_copy(core, t).wait_send()
    for k, dest in far:
        for t, p in steps:
            far_copy(k, core, group, 0, t, p, row).wait_send()

    @pl.when(row == diag_row)
    def _():
        for source in range(groups):
            for child in range(2):
                @pl.when(2 * source + child != row)
                def _():
                    for t in range(col_cap):
                        diag_copy(source, child, t).wait_recv()

    @pl.when(row != diag_row)
    def _():
        for t in range(col_cap):
            diag_copy(group, core, t).wait_send()

    for k, dest in far:
        @pl.when(jnp.logical_not(overlaps(dest)))
        def _():
            for t in range(col_cap):
                col_copy(k, group, t, dest).wait_send()

    @pl.when(holder)
    def _():
        for t, p in steps:
            for k, source in sources:
                z_copy(k, source, 1 - par, 1, t, p).wait_recv()
                xr_copy(k, source, 1 - par, t, p).wait_send()
                for child in range(2):
                    x_copy(k, source, par, child, t, p).wait_send()
                    z_copy(k, source, par, child, t, p).wait_send()

    @pl.when(jnp.logical_not(holder))
    def _():
        for t, p in steps:
            for k, source in sources:
                zr_copy(k, source, par, t, p).wait_send()
                zr_copy(k, source, 1 - par, t, p).wait_recv()
                xr_copy(k, source, 1 - par, t, p).wait_recv()

    @pl.when(overlaps(group))
    def _():
        @pl.when(holder)
        def _():
            for k, source in sources:
                for t in range(col_cap):
                    for child in range(2):
                        over_copy(k, source, child, t).wait_send()

        @pl.when(jnp.logical_not(holder))
        def _():
            for k, source in sources:
                for t in range(col_cap):
                    for child in range(2):
                        over_copy(k, source, child, t).wait_recv()

    @pl.when(jnp.logical_not(overlaps(group)))
    def _():
        for t in range(col_cap):
            for k, source in sources:
                fwd_copy(k, source, 1 - core, t).wait_recv()
                fwd_copy(k, source, core, t).wait_send()


def add_kernel(
    row_count, col_count, front_ref, rows_ref, cols_ref, diag_ref, out_ref, staged, out_sem
):
    rows_local, halves, block, cols_local, _ = front_ref.shape
    _, row_cap, _, _, rank = rows_ref.shape
    col_cap = cols_ref.shape[1]
    ratio = col_count // row_count
    row = lax.axis_index("row")
    col = lax.axis_index("col")

    def write(a, h):
        return pltpu.make_async_copy(staged.at[a, h], out_ref.at[a, :, h], out_sem.at[a, h])

    for a in range(rows_local):
        s, m = divmod(a, row_cap)
        rows = jnp.concatenate([rows_ref[s, m, 0], rows_ref[s, m, 1]], axis=1)
        for b in range(cols_local):
            cols = cols_ref[b // col_cap, b % col_cap].reshape(2 * rank, block)
            tile = jnp.dot(rows, cols, preferred_element_type=jnp.float32)
            spot = pl.ds(b, block, stride=cols_local)
            for h in range(halves):
                src = front_ref.at[a, h].reshape(block * cols_local, LANES)
                dst = staged.at[a, h].reshape(block * cols_local, LANES)
                dst[spot, :] = src[spot, :] + tile[:, h * LANES:(h + 1) * LANES]

        @pl.when((a % ratio) * row_count + row == col)
        def _():
            b = a // ratio
            s, t = divmod(b, col_cap)
            piece = diag_ref[s, 0, t].astype(jnp.float32) + diag_ref[s, 1, t].astype(jnp.float32)
            spot = pl.ds(b, block, stride=cols_local)
            for h in range(halves):
                dst = staged.at[a, h].reshape(block * cols_local, LANES)
                dst[spot, :] = dst[spot, :] + piece[:, h * LANES:(h + 1) * LANES]

        for h in range(halves):
            write(a, h).start()
    for a in range(rows_local):
        for h in range(halves):
            write(a, h).wait()


def shards(parent_front, generators, diagonal_blocks, coupling, block_map, valid_rows):
    row_count = lax.axis_size("row")
    col_count = lax.axis_size("col")
    groups = row_count // 2
    block, rank = generators.shape[1:]
    rows_local = parent_front.shape[0]
    cols_local = parent_front.shape[2]
    row_cap = rows_local // groups
    col_cap = cols_local // groups
    vmem = pl.BlockSpec(memory_space=pltpu.VMEM)
    hbm = pl.BlockSpec(memory_space=pltpu.HBM)
    dma = pltpu.SemaphoreType.DMA
    halves = block // LANES
    split = parent_front.reshape(rows_local, block, cols_local, halves, LANES)
    split = split.transpose(0, 1, 3, 2, 4)
    held = (rows_local, halves, block, cols_local, LANES)
    operands = [
        pltpu.with_memory_space_constraint(x, pltpu.HBM)
        for x in (generators, diagonal_blocks, coupling, block_map, valid_rows, split)
    ]
    far = groups - 1
    pieces = (far, 2, col_cap, PIECES)
    relays = (far, col_cap, PIECES)
    rows, cols, diag, front = pl.pallas_call(
        functools.partial(exchange_kernel, row_count, col_count, row_cap, col_cap),
        out_shape=(
            pltpu.VMEM((groups, row_cap, 2, block, rank), jnp.bfloat16),
            pltpu.VMEM((groups, col_cap, 2, rank, block), jnp.bfloat16),
            pltpu.VMEM((groups, 2, col_cap, block, block), jnp.bfloat16),
            pltpu.VMEM(held, jnp.float32),
        ),
        in_specs=[hbm] * 6,
        out_specs=(vmem,) * 4,
        scratch_shapes=[
            pltpu.VMEM(generators.shape, jnp.bfloat16),
            pltpu.VMEM(diagonal_blocks.shape, jnp.bfloat16),
            pltpu.VMEM(coupling.shape, jnp.bfloat16),
            pltpu.SMEM(block_map.shape, jnp.int32),
            pltpu.SMEM(valid_rows.shape, jnp.int32),
            dma((5,)),
            dma((rows_local, halves)),
            pltpu.VMEM((far, col_cap, block, rank), jnp.bfloat16),
            pltpu.VMEM((row_cap, block, rank), jnp.bfloat16),
            pltpu.VMEM((col_cap, block, block), jnp.bfloat16),
            dma(relays),
            dma(pieces),
            dma(pieces),
            dma(pieces),
            dma(pieces),
            dma(pieces),
            dma(relays),
            dma(relays),
            dma(relays),
            dma(relays),
            dma((row_cap,)),
            dma((row_cap,)),
            dma((col_cap,)),
            dma((col_cap,)),
            dma((far, col_cap)),
            dma((far, col_cap)),
            dma((far, col_cap)),
            dma((far, col_cap)),
            dma((far, 2, col_cap)),
            dma((far, 2, col_cap)),
            dma((col_cap,)),
            dma((groups, 2, col_cap)),
        ],
        compiler_params=pltpu.CompilerParams(
            collective_id=0, has_side_effects=True, vmem_limit_bytes=32 * 1024 * 1024
        ),
    )(*operands)
    out = pl.pallas_call(
        functools.partial(add_kernel, row_count, col_count),
        out_shape=jax.ShapeDtypeStruct(split.shape, jnp.float32),
        in_specs=[vmem] * 4,
        out_specs=hbm,
        scratch_shapes=[pltpu.VMEM(held, jnp.float32), dma((rows_local, halves))],
        compiler_params=pltpu.CompilerParams(vmem_limit_bytes=32 * 1024 * 1024),
    )(*(pltpu.with_memory_space_constraint(x, pltpu.VMEM) for x in (front, rows, cols, diag)))
    return out.transpose(0, 1, 3, 2, 4).reshape(parent_front.shape)


def solution(mesh):
    in_specs = (
        P(None, "row", None, "col"),
        P("row", None, None),
        P("row", None, None),
        P(),
        P(),
        P(),
    )
    out_specs = P(None, "row", None, "col")
    return jax.shard_map(shards, mesh=mesh, in_specs=in_specs, out_specs=out_specs, check_vma=False)
```

time: 31.3 us -> 25.3 us (0.81)
  the two profiles are of different devices: /device:TPU:1 before, /device:TPU:0 now
where the time goes in v1:
time: 25.3 us; the launch traced here: 25.1 us
  Pallas kernels  25.1 us (99%)
    pallas_call x1, Pallas kernels, shards(): pl.pallas_call(functools.partial(exchange_kernel, row_count, col_count, r...  20.3 us
    pallas_call x1, Pallas kernels, shards(): pl.pallas_call(functools.partial(add_kernel, row_count, col_count), out_s...  4.84 us

profile of v1, /device:TPU:0, one launch (start us, length us, event | category | flops | bytes accessed | tf_op | source)
XLA Modules:
  0.0 25.1 jit_solution(15420535730996906733)
XLA Ops:
  0.0 20.3 %shard_map.64 = (bf16[2,4,2,256,256]{4,3,2,1,0:T(8,128)(2,1)S(1)}, bf16[2,2,2,256,256]{4,3,2,1,0:T(8,128)(2,1)S(1)}, bf16[2,2,2,256,256]{4,3,2,1,0:T(8,128)(2,1)S(1)}, f32[8,2,256,4,128]{4,3,2,1,0:T(4,128)S(1)}) custom-call(bf16[12,256,256]{2,1,0:T(8,128)(2,1)} %gen_hbm.1, bf16[12,256,256]{2,1,0:T(8,128)(2,1)} %diag_hbm.1, ...), custom_call_target="tpu_custom_call" | custom-call | tf_op jit(solution)/shard_map/pallas_call | solution.py:397
  20.3 4.8 %shard_map.65 = f32[8,256,2,4,128]{4,3,2,1,0:T(4,128)} custom-call(f32[8,2,256,4,128]{4,3,2,1,0:T(4,128)S(1)} %get-tuple-element.9.front_ref, bf16[2,4,2,256,256]{4,3,2,1,0:T(8,128)(2,1)S(1)} %get-tuple-element.10.rows_ref, bf16[2,2,2,256,256]{4,3,2,1,0:T(8,128)(2,1)S(1)} %get-tuple-element.11.cols_ref, ...), custom_call_target="tpu_custom_call" | custom-call | tf_op jit(solution)/shard_map/pallas_call | solution.py:445

commit v2 on v1

--- a/solution.py
+++ b/solution.py
@@ -10,16 +10,32 @@
 MESH = pl.DeviceIdType.MESH
 QUAD = 4
 LANES = 128
-PIECES = 2
-LAG = 2
+
+
+def steps_of(col_cap, block):
+    unit = block // QUAD
+    steps = []
+    for t in range(col_cap):
+        shape = (2, 2)
+        if col_cap == 1:
+            shape = (1, 1, 1, 1)
+        elif t == 0:
+            shape = (1, 1, 2)
+        elif t == col_cap - 1:
+            shape = (2, 1, 1)
+        start = 0
+        for size in shape:
+            steps.append((t, start * unit, size * unit))
+            start += size
+    return steps
 
 
 def exchange_kernel(
     row_count, col_count, row_cap, col_cap,
     gen_hbm, diag_hbm, coupling_hbm, map_hbm, count_hbm, front_hbm,
-    rows_out, cols_out, diag_out, front_out,
+    rows_out, cols_out, front_out,
     gen_ref, diag_ref, coupling_ref, map_ref, count_ref, load_sem, front_sem,
-    far_rows, pair_rows, own_diag,
+    far_rows, pair_rows, own_diag, diag_in,
     far_send, far_recv, x_send, x_recv, z_send, z_recv, xr_send, xr_recv, zr_send, zr_recv,
     pair_send, pair_recv, near_send, near_recv, col_send, col_recv, fwd_send, fwd_recv,
     over_send, over_recv, diag_send, diag_recv,
@@ -27,8 +43,10 @@
     groups = row_count // 2
     group_blocks, block, rank = gen_ref.shape
     window = row_cap * row_count
-    rows_of = block // PIECES
-    steps = [(t, p) for t in range(col_cap) for p in range(PIECES)]
+    steps = steps_of(col_cap, block)
+    middle = len(steps) // 2
+    ratio = col_count // row_count
+    cols_local = groups * col_cap
     row = lax.axis_index("row")
     col = lax.axis_index("col")
     group = row // 2
@@ -87,7 +105,7 @@
             (coupling_hbm, coupling_ref), (diag_hbm, diag_ref),
         ))
     ]
-    for copy in loads:
+    for copy in loads[:4]:
         copy.start()
 
     barrier = pltpu.get_barrier_semaphore()
@@ -98,35 +116,31 @@
     for other in (x_col, z_col):
         pl.semaphore_signal(barrier, inc=1, device_id=(row, other), device_id_type=MESH)
 
-    def far_copy(k, child, source, par, t, p, dest_row):
-        part = pl.ds(p * rows_of, rows_of)
+    def far_copy(k, child, source, par, i, dest_row):
+        t, start, size = steps[i]
+        part = pl.ds(start, size)
         return remote(
             far_rows.at[k - 1, t, part], rows_out.at[source, 2 * t + par, child, part],
-            far_send.at[k - 1, t, p], far_recv.at[k - 1, child, t, p], dest_row, col,
-        )
-
-    def landed(source, par, child, t, p):
-        return rows_out.at[source, 2 * t + par, child, pl.ds(p * rows_of, rows_of)]
-
-    def x_copy(k, source, par, child, t, p):
-        piece = landed(source, par, child, t, p)
-        at = (k - 1, child, t, p)
-        return remote(piece, piece, x_send.at[at], x_recv.at[at], row, x_col)
-
-    def z_copy(k, source, par, child, t, p):
-        piece = landed(source, par, child, t, p)
-        at = (k - 1, child, t, p)
-        return remote(piece, piece, z_send.at[at], z_recv.at[at], row, z_col)
-
-    def xr_copy(k, source, par, t, p):
-        piece = landed(source, par, 0, t, p)
-        at = (k - 1, t, p)
-        return remote(piece, piece, xr_send.at[at], xr_recv.at[at], row, x_col)
-
-    def zr_copy(k, source, par, t, p):
-        piece = landed(source, par, 1, t, p)
-        at = (k - 1, t, p)
-        return remote(piece, piece, zr_send.at[at], zr_recv.at[at], row, z_col)
+            far_send.at[k - 1, i], far_recv.at[k - 1, child, i], dest_row, col,
+        )
+
+    def piece_copy(k, source, par, child, i, send, recv, to_col):
+        t, start, size = steps[i]
+        piece = rows_out.at[source, 2 * t + par, child, pl.ds(start, size)]
+        at = (k - 1, child, i)
+        return remote(piece, piece, send.at[at], recv.at[at], row, to_col)
+
+    def x_copy(k, source, par, child, i):
+        return piece_copy(k, source, par, child, i, x_send, x_recv, x_col)
+
+    def z_copy(k, source, par, child, i):
+        return piece_copy(k, source, par, child, i, z_send, z_recv, z_col)
+
+    def xr_copy(k, source, par, child, i):
+        return piece_copy(k, source, par, child, i, xr_send, xr_recv, x_col)
+
+    def zr_copy(k, source, par, child, i):
+        return piece_copy(k, source, par, child, i, zr_send, zr_recv, z_col)
 
     def pair_copy(child, m):
         return remote(
@@ -155,7 +169,7 @@
 
     def diag_copy(source, child, t):
         return remote(
-            own_diag.at[t], diag_out.at[source, child, t],
+            own_diag.at[t], diag_in.at[source, child, t],
             diag_send.at[t], diag_recv.at[source, child, t], diag_row, col,
         )
 
@@ -165,15 +179,17 @@
 
     for copy in loads[:3]:
         copy.wait()
+    loads[4].start()
     for t in range(col_cap):
         for k, dest in far:
             slot = (2 * t + parity(dest)) * row_count + 2 * dest + quarter % 2
             far_rows[k - 1, t] = masked_rows(slot)
         if t == 0:
             pl.semaphore_wait(barrier, row_count + 1)
-        for k, dest in far:
-            for p in range(PIECES):
-                far_copy(k, core, group, parity(dest), t, p, 2 * dest + quarter % 2).start()
+        for i in range(len(steps)):
+            if steps[i][0] == t:
+                for k, dest in far:
+                    far_copy(k, core, group, parity(dest), i, 2 * dest + quarter % 2).start()
 
     front_loads = [
         pltpu.make_async_copy(front_hbm.at[a, :, h], front_out.at[a, h], front_sem.at[a, h])
@@ -204,7 +220,7 @@
 
         @pl.when(row == diag_row)
         def _():
-            diag_out[group, core, t] = own_diag[t]
+            diag_in[group, core, t] = own_diag[t]
 
     for copy in front_loads:
         copy.start()
@@ -214,39 +230,46 @@
     for m in range(row_cap):
         rows_out[group, m, core] = masked_rows(m * row_count + row)
 
+    def add_diag(source):
+        for t in range(col_cap):
+            b = source * col_cap + t
+            total = diag_in[source, 0, t].astype(jnp.float32) + diag_in[source, 1, t].astype(jnp.float32)
+            spot = pl.ds(b % cols_local, block, stride=cols_local)
+            for h in range(block // LANES):
+                held = front_out.at[b * ratio + half, h].reshape(block * cols_local, LANES)
+                held[spot, :] = held[spot, :] + total[:, h * LANES:(h + 1) * LANES]
+
     @pl.when(holder)
     def _():
-        for i in range(len(steps) + LAG):
-            if i < len(steps):
-                t, p = steps[i]
-                for k, source in sources:
+        for i in range(len(steps)):
+            for k, source in sources:
+                for child in range(2):
+                    far_copy(k, child, source, par, i, row).wait_recv()
+                    x_copy(k, source, par, child, i).start()
+                    z_copy(k, source, par, child, i).start()
+        for i in range(middle):
+            for k, source in sources:
+                for child in range(2):
+                    z_copy(k, source, 1 - par, child, i).wait_recv()
+                    xr_copy(k, source, 1 - par, child, i).start()
+
+        @pl.when(overlaps(group))
+        def _():
+            for k, source in sources:
+                for t in range(col_cap):
                     for child in range(2):
-                        far_copy(k, child, source, par, t, p, row).wait_recv()
-                        x_copy(k, source, par, child, t, p).start()
-                        z_copy(k, source, par, child, t, p).start()
-            if i >= LAG:
-                t, p = steps[i - LAG]
-                for k, source in sources:
-                    z_copy(k, source, 1 - par, 0, t, p).wait_recv()
-                    xr_copy(k, source, 1 - par, t, p).start()
-            if i == len(steps) - 1:
-                @pl.when(overlaps(group))
-                def _():
-                    for k, source in sources:
-                        for t in range(col_cap):
-                            for child in range(2):
-                                cols_out[source, t, child] = project(
-                                    child, rows_out[source, 2 * t + par, child]
-                                )
-                                over_copy(k, source, child, t).start()
+                        cols_out[source, t, child] = project(
+                            child, rows_out[source, 2 * t + par, child]
+                        )
+                        over_copy(k, source, child, t).start()
 
     @pl.when(jnp.logical_not(holder))
     def _():
-        for t, p in steps:
-            for k, source in sources:
-                x_copy(k, source, par, 1, t, p).wait_recv()
-                zr_copy(k, source, par, t, p).start()
-                x_copy(k, source, par, 0, t, p).wait_recv()
+        for i in range(middle, len(steps)):
+            for k, source in sources:
+                for child in range(2):
+                    x_copy(k, source, par, child, i).wait_recv()
+                    zr_copy(k, source, par, child, i).start()
 
     @pl.when(jnp.logical_not(overlaps(group)))
     def _():
@@ -257,6 +280,13 @@
 
     for copy in front_loads:
         copy.wait()
+
+    @pl.when(row == diag_row)
+    def _():
+        for t in range(col_cap):
+            diag_copy(group, 1 - core, t).wait_recv()
+        add_diag(group)
+
     for m in range(row_cap):
         pair_copy(1 - core, m).wait_recv()
         pair_copy(core, m).wait_send()
@@ -264,17 +294,16 @@
         near_copy(1 - core, t).wait_recv()
         near_copy(core, t).wait_send()
     for k, dest in far:
-        for t, p in steps:
-            far_copy(k, core, group, 0, t, p, row).wait_send()
+        for i in range(len(steps)):
+            far_copy(k, core, group, 0, i, row).wait_send()
 
     @pl.when(row == diag_row)
     def _():
-        for source in range(groups):
+        for k, source in sources:
             for child in range(2):
-                @pl.when(2 * source + child != row)
-                def _():
-                    for t in range(col_cap):
-                        diag_copy(source, child, t).wait_recv()
+                for t in range(col_cap):
+                    diag_copy(source, child, t).wait_recv()
+            add_diag(source)
 
     @pl.when(row != diag_row)
     def _():
@@ -289,21 +318,27 @@
 
     @pl.when(holder)
     def _():
-        for t, p in steps:
-            for k, source in sources:
-                z_copy(k, source, 1 - par, 1, t, p).wait_recv()
-                xr_copy(k, source, 1 - par, t, p).wait_send()
-                for child in range(2):
-                    x_copy(k, source, par, child, t, p).wait_send()
-                    z_copy(k, source, par, child, t, p).wait_send()
+        for k, source in sources:
+            for child in range(2):
+                for i in range(len(steps)):
+                    if i >= middle:
+                        z_copy(k, source, 1 - par, child, i).wait_recv()
+                    else:
+                        xr_copy(k, source, 1 - par, child, i).wait_send()
+                    x_copy(k, source, par, child, i).wait_send()
+                    z_copy(k, source, par, child, i).wait_send()
 
     @pl.when(jnp.logical_not(holder))
     def _():
-        for t, p in steps:
-            for k, source in sources:
-                zr_copy(k, source, par, t, p).wait_send()
-                zr_copy(k, source, 1 - par, t, p).wait_recv()
-                xr_copy(k, source, 1 - par, t, p).wait_recv()
+        for k, source in sources:
+            for child in range(2):
+                for i in range(len(steps)):
+                    if i >= middle:
+                        zr_copy(k, source, par, child, i).wait_send()
+                        zr_copy(k, source, 1 - par, child, i).wait_recv()
+                    else:
+                        x_copy(k, source, par, child, i).wait_recv()
+                        xr_copy(k, source, 1 - par, child, i).wait_recv()
 
     @pl.when(overlaps(group))
     def _():
@@ -330,14 +365,11 @@
 
 
 def add_kernel(
-    row_count, col_count, front_ref, rows_ref, cols_ref, diag_ref, out_ref, staged, out_sem
+    front_ref, rows_ref, cols_ref, out_ref, staged, out_sem
 ):
     rows_local, halves, block, cols_local, _ = front_ref.shape
     _, row_cap, _, _, rank = rows_ref.shape
     col_cap = cols_ref.shape[1]
-    ratio = col_count // row_count
-    row = lax.axis_index("row")
-    col = lax.axis_index("col")
 
     def write(a, h):
         return pltpu.make_async_copy(staged.at[a, h], out_ref.at[a, :, h], out_sem.at[a, h])
@@ -353,16 +385,6 @@
                 src = front_ref.at[a, h].reshape(block * cols_local, LANES)
                 dst = staged.at[a, h].reshape(block * cols_local, LANES)
                 dst[spot, :] = src[spot, :] + tile[:, h * LANES:(h + 1) * LANES]
-
-        @pl.when((a % ratio) * row_count + row == col)
-        def _():
-            b = a // ratio
-            s, t = divmod(b, col_cap)
-            piece = diag_ref[s, 0, t].astype(jnp.float32) + diag_ref[s, 1, t].astype(jnp.float32)
-            spot = pl.ds(b, block, stride=cols_local)
-            for h in range(halves):
-                dst = staged.at[a, h].reshape(block * cols_local, LANES)
-                dst[spot, :] = dst[spot, :] + piece[:, h * LANES:(h + 1) * LANES]
 
         for h in range(halves):
             write(a, h).start()
@@ -392,18 +414,16 @@
         for x in (generators, diagonal_blocks, coupling, block_map, valid_rows, split)
     ]
     far = groups - 1
-    pieces = (far, 2, col_cap, PIECES)
-    relays = (far, col_cap, PIECES)
-    rows, cols, diag, front = pl.pallas_call(
+    pieces = (far, 2, len(steps_of(col_cap, block)))
+    rows, cols, front = pl.pallas_call(
         functools.partial(exchange_kernel, row_count, col_count, row_cap, col_cap),
         out_shape=(
             pltpu.VMEM((groups, row_cap, 2, block, rank), jnp.bfloat16),
             pltpu.VMEM((groups, col_cap, 2, rank, block), jnp.bfloat16),
-            pltpu.VMEM((groups, 2, col_cap, block, block), jnp.bfloat16),
             pltpu.VMEM(held, jnp.float32),
         ),
         in_specs=[hbm] * 6,
-        out_specs=(vmem,) * 4,
+        out_specs=(vmem,) * 3,
         scratch_shapes=[
             pltpu.VMEM(generators.shape, jnp.bfloat16),
             pltpu.VMEM(diagonal_blocks.shape, jnp.bfloat16),
@@ -415,16 +435,17 @@
             pltpu.VMEM((far, col_cap, block, rank), jnp.bfloat16),
             pltpu.VMEM((row_cap, block, rank), jnp.bfloat16),
             pltpu.VMEM((col_cap, block, block), jnp.bfloat16),
-            dma(relays),
-            dma(pieces),
-            dma(pieces),
-            dma(pieces),
-            dma(pieces),
-            dma(pieces),
-            dma(relays),
-            dma(relays),
-            dma(relays),
-            dma(relays),
+            pltpu.VMEM((groups, 2, col_cap, block, block), jnp.bfloat16),
+            dma((far, len(steps_of(col_cap, block)))),
+            dma(pieces),
+            dma(pieces),
+            dma(pieces),
+            dma(pieces),
+            dma(pieces),
+            dma(pieces),
+            dma(pieces),
+            dma(pieces),
+            dma(pieces),
             dma((row_cap,)),
             dma((row_cap,)),
             dma((col_cap,)),
@@ -443,13 +464,13 @@
         ),
     )(*operands)
     out = pl.pallas_call(
-        functools.partial(add_kernel, row_count, col_count),
+        add_kernel,
         out_shape=jax.ShapeDtypeStruct(split.shape, jnp.float32),
-        in_specs=[vmem] * 4,
+        in_specs=[vmem] * 3,
         out_specs=hbm,
         scratch_shapes=[pltpu.VMEM(held, jnp.float32), dma((rows_local, halves))],
         compiler_params=pltpu.CompilerParams(vmem_limit_bytes=32 * 1024 * 1024),
-    )(*(pltpu.with_memory_space_constraint(x, pltpu.VMEM) for x in (front, rows, cols, diag)))
+    )(*(pltpu.with_memory_space_constraint(x, pltpu.VMEM) for x in (front, rows, cols)))
     return out.transpose(0, 1, 3, 2, 4).reshape(parent_front.shape)
 
 

time: 25.3 us -> 24 us (0.949)
  the two profiles are of different devices: /device:TPU:0 before, /device:TPU:1 now
where the time goes in v2:
time: 24 us; the launch traced here: 23.8 us
  Pallas kernels  23.8 us (99%)
    pallas_call x1, Pallas kernels, shards(): pl.pallas_call(functools.partial(exchange_kernel, row_count, col_count, r...  19.9 us
    pallas_call x1, Pallas kernels, shards(): pl.pallas_call(add_kernel, out_shape=jax.ShapeDtypeStruct(split.shape, jn...  3.86 us

profile of v2, /device:TPU:1, one launch (start us, length us, event | category | flops | bytes accessed | tf_op | source)
XLA Modules:
  0.0 23.8 jit_solution(1163427079765110826)
XLA Ops:
  0.0 19.9 %shard_map.64 = (bf16[2,4,2,256,256]{4,3,2,1,0:T(8,128)(2,1)S(1)}, bf16[2,2,2,256,256]{4,3,2,1,0:T(8,128)(2,1)S(1)}, f32[8,2,256,4,128]{4,3,2,1,0:T(4,128)S(1)}) custom-call(bf16[12,256,256]{2,1,0:T(8,128)(2,1)} %gen_hbm.1, bf16[12,256,256]{2,1,0:T(8,128)(2,1)} %diag_hbm.1, bf16[2,256,256]{2,1,0:T(8,128)(2,1)} %coupling_hbm.1, s32[2,24]{1,0:T(2,128)} %map_hbm.1, ...), custom_call_target="tpu_custom_call" | custom-call | tf_op jit(solution)/shard_map/pallas_call | solution.py:418
  19.9 3.9 %shard_map.65 = f32[8,256,2,4,128]{4,3,2,1,0:T(4,128)} custom-call(f32[8,2,256,4,128]{4,3,2,1,0:T(4,128)S(1)} %get-tuple-element.8.front_ref, bf16[2,4,2,256,256]{4,3,2,1,0:T(8,128)(2,1)S(1)} %get-tuple-element.9.rows_ref, bf16[2,2,2,256,256]{4,3,2,1,0:T(8,128)(2,1)S(1)} %get-tuple-element.10.cols_ref), custom_call_target="tpu_custom_call" | custom-call | tf_op jit(solution)/shard_map/pallas_call | solution.py:466

commit v3 on v2

--- a/solution.py
+++ b/solution.py
@@ -13,21 +13,9 @@
 
 
 def steps_of(col_cap, block):
-    unit = block // QUAD
-    steps = []
-    for t in range(col_cap):
-        shape = (2, 2)
-        if col_cap == 1:
-            shape = (1, 1, 1, 1)
-        elif t == 0:
-            shape = (1, 1, 2)
-        elif t == col_cap - 1:
-            shape = (2, 1, 1)
-        start = 0
-        for size in shape:
-            steps.append((t, start * unit, size * unit))
-            start += size
-    return steps
+    per_block = QUAD // col_cap
+    size = block // per_block
+    return [(t, p * size, size) for t in range(col_cap) for p in range(per_block)]
 
 
 def exchange_kernel(
@@ -36,9 +24,9 @@
     rows_out, cols_out, front_out,
     gen_ref, diag_ref, coupling_ref, map_ref, count_ref, load_sem, front_sem,
     far_rows, pair_rows, own_diag, diag_in,
-    far_send, far_recv, x_send, x_recv, z_send, z_recv, xr_send, xr_recv, zr_send, zr_recv,
-    pair_send, pair_recv, near_send, near_recv, col_send, col_recv, fwd_send, fwd_recv,
-    over_send, over_recv, diag_send, diag_recv,
+    far_send, far_recv, x_send, z_send, step_recv, relay_send, relay_recv,
+    pair_send, pair_recv, near_send, near_recv, col_send, col_recv, side_send, side_recv,
+    diag_send, diag_recv,
 ):
     groups = row_count // 2
     group_blocks, block, rank = gen_ref.shape
@@ -121,56 +109,59 @@
         part = pl.ds(start, size)
         return remote(
             far_rows.at[k - 1, t, part], rows_out.at[source, 2 * t + par, child, part],
-            far_send.at[k - 1, i], far_recv.at[k - 1, child, i], dest_row, col,
-        )
-
-    def piece_copy(k, source, par, child, i, send, recv, to_col):
+            far_send.at[k - 1], far_recv.at[k - 1, i], dest_row, col,
+        )
+
+    def piece_copy(source, par, i, send, recv, to_col):
         t, start, size = steps[i]
-        piece = rows_out.at[source, 2 * t + par, child, pl.ds(start, size)]
-        at = (k - 1, child, i)
-        return remote(piece, piece, send.at[at], recv.at[at], row, to_col)
-
-    def x_copy(k, source, par, child, i):
-        return piece_copy(k, source, par, child, i, x_send, x_recv, x_col)
-
-    def z_copy(k, source, par, child, i):
-        return piece_copy(k, source, par, child, i, z_send, z_recv, z_col)
-
-    def xr_copy(k, source, par, child, i):
-        return piece_copy(k, source, par, child, i, xr_send, xr_recv, x_col)
-
-    def zr_copy(k, source, par, child, i):
-        return piece_copy(k, source, par, child, i, zr_send, zr_recv, z_col)
+        piece = rows_out.at[source, 2 * t + par, :, pl.ds(start, size)]
+        return remote(piece, piece, send, recv, row, to_col)
+
+    def far_landed(k, source, par, i):
+        return piece_copy(source, par, i, far_send.at[k - 1], far_recv.at[k - 1, i], col)
+
+    def x_copy(k, source, par, i):
+        return piece_copy(source, par, i, x_send.at[k - 1], step_recv.at[k - 1, i], x_col)
+
+    def z_copy(k, source, par, i):
+        return piece_copy(source, par, i, z_send.at[k - 1], step_recv.at[k - 1, i], z_col)
+
+    def xr_copy(k, source, par, i):
+        return piece_copy(source, par, i, relay_send.at[k - 1], relay_recv.at[k - 1], x_col)
+
+    def zr_copy(k, source, par, i):
+        return piece_copy(source, par, i, relay_send.at[k - 1], relay_recv.at[k - 1], z_col)
+
+    def all_of(ref, send, recv):
+        return remote(ref, ref, send, recv, pair_row, col)
 
     def pair_copy(child, m):
         return remote(
-            pair_rows.at[m], rows_out.at[group, m, child],
-            pair_send.at[m], pair_recv.at[m], pair_row, col,
+            pair_rows.at[m], rows_out.at[group, m, child], pair_send, pair_recv, pair_row, col
         )
 
     def near_copy(child, t):
         piece = cols_out.at[group, t, child]
-        return remote(piece, piece, near_send.at[t], near_recv.at[t], pair_row, col)
+        return remote(piece, piece, near_send, near_recv, pair_row, col)
 
     def col_copy(k, source, t, dest):
         piece = cols_out.at[source, t, core]
         return remote(
-            piece, piece, col_send.at[k - 1, t], col_recv.at[k - 1, t], 2 * dest + core, col
-        )
-
-    def fwd_copy(k, source, child, t):
-        piece = cols_out.at[source, t, child]
-        return remote(piece, piece, fwd_send.at[k - 1, t], fwd_recv.at[k - 1, t], pair_row, col)
-
-    def over_copy(k, source, child, t):
-        piece = cols_out.at[source, t, child]
-        at = (k - 1, child, t)
-        return remote(piece, piece, over_send.at[at], over_recv.at[at], pair_row, col)
-
-    def diag_copy(source, child, t):
+            piece, piece, col_send.at[k - 1], col_recv.at[k - 1, t], 2 * dest + core, col
+        )
+
+    def fwd_copy(k, source, t):
+        piece = cols_out.at[source, t, core]
+        return remote(piece, piece, side_send.at[k - 1], side_recv.at[k - 1], pair_row, col)
+
+    def over_copy(k, source, t):
+        piece = cols_out.at[source, t]
+        return remote(piece, piece, side_send.at[k - 1], side_recv.at[k - 1], pair_row, col)
+
+    def diag_copy(t):
         return remote(
-            own_diag.at[t], diag_in.at[source, child, t],
-            diag_send.at[t], diag_recv.at[source, child, t], diag_row, col,
+            own_diag.at[t], diag_in.at[group, core, t], diag_send, diag_recv.at[group],
+            diag_row, col,
         )
 
     far = [(k, (group + k) % groups) for k in range(1, groups)]
@@ -192,8 +183,8 @@
                     far_copy(k, core, group, parity(dest), i, 2 * dest + quarter % 2).start()
 
     front_loads = [
-        pltpu.make_async_copy(front_hbm.at[a, :, h], front_out.at[a, h], front_sem.at[a, h])
-        for a in range(front_out.shape[0]) for h in range(front_out.shape[1])
+        pltpu.make_async_copy(front_hbm.at[:, :, h], front_out.at[:, h], front_sem.at[h])
+        for h in range(front_out.shape[1])
     ]
     for copy in loads[3:]:
         copy.wait()
@@ -216,7 +207,7 @@
 
         @pl.when(row != diag_row)
         def _():
-            diag_copy(group, core, t).start()
+            diag_copy(t).start()
 
         @pl.when(row == diag_row)
         def _():
@@ -243,15 +234,13 @@
     def _():
         for i in range(len(steps)):
             for k, source in sources:
-                for child in range(2):
-                    far_copy(k, child, source, par, i, row).wait_recv()
-                    x_copy(k, source, par, child, i).start()
-                    z_copy(k, source, par, child, i).start()
+                far_landed(k, source, par, i).wait_recv()
+                x_copy(k, source, par, i).start()
+                z_copy(k, source, par, i).start()
         for i in range(middle):
             for k, source in sources:
-                for child in range(2):
-                    z_copy(k, source, 1 - par, child, i).wait_recv()
-                    xr_copy(k, source, 1 - par, child, i).start()
+                z_copy(k, source, 1 - par, i).wait_recv()
+                xr_copy(k, source, 1 - par, i).start()
 
         @pl.when(overlaps(group))
         def _():
@@ -261,107 +250,91 @@
                         cols_out[source, t, child] = project(
                             child, rows_out[source, 2 * t + par, child]
                         )
-                        over_copy(k, source, child, t).start()
+                    over_copy(k, source, t).start()
 
     @pl.when(jnp.logical_not(holder))
     def _():
         for i in range(middle, len(steps)):
             for k, source in sources:
-                for child in range(2):
-                    x_copy(k, source, par, child, i).wait_recv()
-                    zr_copy(k, source, par, child, i).start()
+                x_copy(k, source, par, i).wait_recv()
+                zr_copy(k, source, par, i).start()
 
     @pl.when(jnp.logical_not(overlaps(group)))
     def _():
         for t in range(col_cap):
             for k, source in sources:
                 col_copy(k, source, t, group).wait_recv()
-                fwd_copy(k, source, core, t).start()
+                fwd_copy(k, source, t).start()
 
     for copy in front_loads:
         copy.wait()
 
     @pl.when(row == diag_row)
     def _():
-        for t in range(col_cap):
-            diag_copy(group, 1 - core, t).wait_recv()
+        all_of(diag_in.at[group, 1 - core], diag_send, diag_recv.at[group]).wait_recv()
         add_diag(group)
 
-    for m in range(row_cap):
-        pair_copy(1 - core, m).wait_recv()
-        pair_copy(core, m).wait_send()
-    for t in range(col_cap):
-        near_copy(1 - core, t).wait_recv()
-        near_copy(core, t).wait_send()
+    all_of(pair_rows, pair_send, pair_recv).wait_recv()
+    all_of(pair_rows, pair_send, pair_recv).wait_send()
+    all_of(cols_out.at[group, :, 1 - core], near_send, near_recv).wait_recv()
+    all_of(cols_out.at[group, :, core], near_send, near_recv).wait_send()
     for k, dest in far:
-        for i in range(len(steps)):
-            far_copy(k, core, group, 0, i, row).wait_send()
-
-    @pl.when(row == diag_row)
-    def _():
-        for k, source in sources:
-            for child in range(2):
-                for t in range(col_cap):
-                    diag_copy(source, child, t).wait_recv()
-            add_diag(source)
+        all_of(far_rows.at[k - 1], far_send.at[k - 1], relay_recv.at[k - 1]).wait_send()
 
     @pl.when(row != diag_row)
     def _():
-        for t in range(col_cap):
-            diag_copy(group, core, t).wait_send()
+        all_of(own_diag, diag_send, diag_recv.at[group]).wait_send()
 
     for k, dest in far:
         @pl.when(jnp.logical_not(overlaps(dest)))
         def _():
-            for t in range(col_cap):
-                col_copy(k, group, t, dest).wait_send()
+            all_of(cols_out.at[group, :, core], col_send.at[k - 1], side_recv.at[k - 1]).wait_send()
+
+    @pl.when(row == diag_row)
+    def _():
+        for k, source in sources:
+            all_of(diag_in.at[source], diag_send, diag_recv.at[source]).wait_recv()
+            add_diag(source)
+
+    one_part = rows_out.at[group, pl.ds(0, col_cap)]
+    half_part = rows_out.at[group, pl.ds(0, col_cap), 0]
 
     @pl.when(holder)
     def _():
         for k, source in sources:
-            for child in range(2):
-                for i in range(len(steps)):
-                    if i >= middle:
-                        z_copy(k, source, 1 - par, child, i).wait_recv()
-                    else:
-                        xr_copy(k, source, 1 - par, child, i).wait_send()
-                    x_copy(k, source, par, child, i).wait_send()
-                    z_copy(k, source, par, child, i).wait_send()
+            for i in range(middle, len(steps)):
+                z_copy(k, source, 1 - par, i).wait_recv()
+            all_of(one_part, x_send.at[k - 1], relay_recv.at[k - 1]).wait_send()
+            all_of(one_part, z_send.at[k - 1], relay_recv.at[k - 1]).wait_send()
+            all_of(half_part, relay_send.at[k - 1], relay_recv.at[k - 1]).wait_send()
 
     @pl.when(jnp.logical_not(holder))
     def _():
         for k, source in sources:
-            for child in range(2):
-                for i in range(len(steps)):
-                    if i >= middle:
-                        zr_copy(k, source, par, child, i).wait_send()
-                        zr_copy(k, source, 1 - par, child, i).wait_recv()
-                    else:
-                        x_copy(k, source, par, child, i).wait_recv()
-                        xr_copy(k, source, 1 - par, child, i).wait_recv()
+            for i in range(middle):
+                x_copy(k, source, par, i).wait_recv()
+            all_of(half_part, relay_send.at[k - 1], relay_recv.at[k - 1]).wait_send()
+            all_of(one_part, relay_send.at[k - 1], relay_recv.at[k - 1]).wait_recv()
 
     @pl.when(overlaps(group))
     def _():
-        @pl.when(holder)
-        def _():
-            for k, source in sources:
-                for t in range(col_cap):
-                    for child in range(2):
-                        over_copy(k, source, child, t).wait_send()
-
-        @pl.when(jnp.logical_not(holder))
-        def _():
-            for k, source in sources:
-                for t in range(col_cap):
-                    for child in range(2):
-                        over_copy(k, source, child, t).wait_recv()
+        for k, source in sources:
+            moved = all_of(cols_out.at[source], side_send.at[k - 1], side_recv.at[k - 1])
+
+            @pl.when(holder)
+            def _():
+                moved.wait_send()
+
+            @pl.when(jnp.logical_not(holder))
+            def _():
+                moved.wait_recv()
 
     @pl.when(jnp.logical_not(overlaps(group)))
     def _():
-        for t in range(col_cap):
-            for k, source in sources:
-                fwd_copy(k, source, 1 - core, t).wait_recv()
-                fwd_copy(k, source, core, t).wait_send()
+        for k, source in sources:
+            moved = all_of(cols_out.at[source, :, core], side_send.at[k - 1], side_recv.at[k - 1])
+            moved.wait_recv()
+            moved.wait_send()
 
 
 def add_kernel(
@@ -372,7 +345,7 @@
     col_cap = cols_ref.shape[1]
 
     def write(a, h):
-        return pltpu.make_async_copy(staged.at[a, h], out_ref.at[a, :, h], out_sem.at[a, h])
+        return pltpu.make_async_copy(staged.at[a, h], out_ref.at[a, :, h], out_sem)
 
     for a in range(rows_local):
         s, m = divmod(a, row_cap)
@@ -388,9 +361,7 @@
 
         for h in range(halves):
             write(a, h).start()
-    for a in range(rows_local):
-        for h in range(halves):
-            write(a, h).wait()
+    pltpu.make_async_copy(staged, staged, out_sem).wait()
 
 
 def shards(parent_front, generators, diagonal_blocks, coupling, block_map, valid_rows):
@@ -414,7 +385,6 @@
         for x in (generators, diagonal_blocks, coupling, block_map, valid_rows, split)
     ]
     far = groups - 1
-    pieces = (far, 2, len(steps_of(col_cap, block)))
     rows, cols, front = pl.pallas_call(
         functools.partial(exchange_kernel, row_count, col_count, row_cap, col_cap),
         out_shape=(
@@ -431,33 +401,28 @@
             pltpu.SMEM(block_map.shape, jnp.int32),
             pltpu.SMEM(valid_rows.shape, jnp.int32),
             dma((5,)),
-            dma((rows_local, halves)),
+            dma((halves,)),
             pltpu.VMEM((far, col_cap, block, rank), jnp.bfloat16),
             pltpu.VMEM((row_cap, block, rank), jnp.bfloat16),
             pltpu.VMEM((col_cap, block, block), jnp.bfloat16),
             pltpu.VMEM((groups, 2, col_cap, block, block), jnp.bfloat16),
-            dma((far, len(steps_of(col_cap, block)))),
-            dma(pieces),
-            dma(pieces),
-            dma(pieces),
-            dma(pieces),
-            dma(pieces),
-            dma(pieces),
-            dma(pieces),
-            dma(pieces),
-            dma(pieces),
-            dma((row_cap,)),
-            dma((row_cap,)),
-            dma((col_cap,)),
-            dma((col_cap,)),
+            dma((far,)),
+            dma((far, QUAD)),
+            dma((far,)),
+            dma((far,)),
+            dma((far, QUAD)),
+            dma((far,)),
+            dma((far,)),
+            dma,
+            dma,
+            dma,
+            dma,
+            dma((far,)),
             dma((far, col_cap)),
-            dma((far, col_cap)),
-            dma((far, col_cap)),
-            dma((far, col_cap)),
-            dma((far, 2, col_cap)),
-            dma((far, 2, col_cap)),
-            dma((col_cap,)),
-            dma((groups, 2, col_cap)),
+            dma((far,)),
+            dma((far,)),
+            dma,
+            dma((groups,)),
         ],
         compiler_params=pltpu.CompilerParams(
             collective_id=0, has_side_effects=True, vmem_limit_bytes=32 * 1024 * 1024
@@ -468,7 +433,7 @@
         out_shape=jax.ShapeDtypeStruct(split.shape, jnp.float32),
         in_specs=[vmem] * 3,
         out_specs=hbm,
-        scratch_shapes=[pltpu.VMEM(held, jnp.float32), dma((rows_local, halves))],
+        scratch_shapes=[pltpu.VMEM(held, jnp.float32), dma],
         compiler_params=pltpu.CompilerParams(vmem_limit_bytes=32 * 1024 * 1024),
     )(*(pltpu.with_memory_space_constraint(x, pltpu.VMEM) for x in (front, rows, cols)))
     return out.transpose(0, 1, 3, 2, 4).reshape(parent_front.shape)

time: 24 us -> 22.9 us (0.954)
  Pallas kernels: 23.8 us -> 22.7 us
    pallas_call x1, Pallas kernels: 19.9 us -> 19 us  [shards(): pl.pallas_call(functools.partial(exchange_kernel, row_count, col_count, r...]
where the time goes in v3:
time: 22.9 us; the launch traced here: 22.8 us
  Pallas kernels  22.7 us (99%)
    pallas_call x1, Pallas kernels, shards(): pl.pallas_call(functools.partial(exchange_kernel, row_count, col_count, r...  19 us
    pallas_call x1, Pallas kernels, shards(): pl.pallas_call(add_kernel, out_shape=jax.ShapeDtypeStruct(split.shape, jn...  3.73 us

profile of v3, /device:TPU:1, one launch (start us, length us, event | category | flops | bytes accessed | tf_op | source)
XLA Modules:
  0.0 22.8 jit_solution(8547831945287047888)
XLA Ops:
  0.0 19.0 %shard_map.64 = (bf16[2,4,2,256,256]{4,3,2,1,0:T(8,128)(2,1)S(1)}, bf16[2,2,2,256,256]{4,3,2,1,0:T(8,128)(2,1)S(1)}, f32[8,2,256,4,128]{4,3,2,1,0:T(4,128)S(1)}) custom-call(bf16[12,256,256]{2,1,0:T(8,128)(2,1)} %gen_hbm.1, bf16[12,256,256]{2,1,0:T(8,128)(2,1)} %diag_hbm.1, bf16[2,256,256]{2,1,0:T(8,128)(2,1)} %coupling_hbm.1, s32[2,24]{1,0:T(2,128)} %map_hbm.1, ...), custom_call_target="tpu_custom_call" | custom-call | tf_op jit(solution)/shard_map/pallas_call | solution.py:388
  19.0 3.7 %shard_map.65 = f32[8,256,2,4,128]{4,3,2,1,0:T(4,128)} custom-call(f32[8,2,256,4,128]{4,3,2,1,0:T(4,128)S(1)} %get-tuple-element.8.front_ref, bf16[2,4,2,256,256]{4,3,2,1,0:T(8,128)(2,1)S(1)} %get-tuple-element.9.rows_ref, bf16[2,2,2,256,256]{4,3,2,1,0:T(8,128)(2,1)S(1)} %get-tuple-element.10.cols_ref), custom_call_target="tpu_custom_call" | custom-call | tf_op jit(solution)/shard_map/pallas_call | solution.py:431

commit v4 on v3

--- a/solution.py
+++ b/solution.py
@@ -9,11 +9,12 @@
 
 MESH = pl.DeviceIdType.MESH
 QUAD = 4
+STEPS = 16
 LANES = 128
 
 
 def steps_of(col_cap, block):
-    per_block = QUAD // col_cap
+    per_block = STEPS // col_cap
     size = block // per_block
     return [(t, p * size, size) for t in range(col_cap) for p in range(per_block)]
 
@@ -23,16 +24,22 @@
     gen_hbm, diag_hbm, coupling_hbm, map_hbm, count_hbm, front_hbm,
     rows_out, cols_out, front_out,
     gen_ref, diag_ref, coupling_ref, map_ref, count_ref, load_sem, front_sem,
-    far_rows, pair_rows, own_diag, diag_in,
+    far_rows, extra_rows, pair_rows, own_diag, swap_diag, sum_diag, diag_in,
     far_send, far_recv, x_send, z_send, step_recv, relay_send, relay_recv,
     pair_send, pair_recv, near_send, near_recv, col_send, col_recv, side_send, side_recv,
-    diag_send, diag_recv,
+    swap_send, swap_recv, diag_send, diag_recv, extra_send, extra_recv,
 ):
     groups = row_count // 2
     group_blocks, block, rank = gen_ref.shape
     window = row_cap * row_count
     steps = steps_of(col_cap, block)
     middle = len(steps) // 2
+    first = middle // 2
+    part_rows = col_cap * block // 2
+    if col_cap == 1:
+        extras = [(0, part_rows, part_rows)]
+    else:
+        extras = [(t, 0, block) for t in range(col_cap // 2, col_cap)]
     ratio = col_count // row_count
     cols_local = groups * col_cap
     row = lax.axis_index("row")
@@ -53,6 +60,8 @@
     def overlaps(dest):
         return diag_row // 2 == dest
 
+    z_over = (z_col % row_count) // 2 == group
+
     def lookup(child, source, slot):
         found = jnp.int32(0)
         count = jnp.int32(0)
@@ -158,10 +167,16 @@
         piece = cols_out.at[source, t]
         return remote(piece, piece, side_send.at[k - 1], side_recv.at[k - 1], pair_row, col)
 
-    def diag_copy(t):
+    def swap_copy():
         return remote(
-            own_diag.at[t], diag_in.at[group, core, t], diag_send, diag_recv.at[group],
-            diag_row, col,
+            own_diag.at[pl.ds((1 - core) * part_rows, part_rows)], swap_diag,
+            swap_send, swap_recv, pair_row, col,
+        )
+
+    def diag_copy():
+        return remote(
+            sum_diag, diag_in.at[group, pl.ds(core * part_rows, part_rows)],
+            diag_send, diag_recv.at[group], diag_row, col,
         )
 
     far = [(k, (group + k) % groups) for k in range(1, groups)]
@@ -181,6 +196,18 @@
             if steps[i][0] == t:
                 for k, dest in far:
                     far_copy(k, core, group, parity(dest), i, 2 * dest + quarter % 2).start()
+    for k, dest in far:
+        @pl.when(overlaps(dest))
+        def _():
+            for n, (t, start, size) in enumerate(extras):
+                slot = (2 * t + 1 - parity(dest)) * row_count + 2 * dest + 1 - quarter % 2
+                extra_rows[n] = masked_rows(slot)[start:start + size]
+                copy = remote(
+                    extra_rows.at[n],
+                    rows_out.at[group, 2 * t + 1 - parity(dest), core, pl.ds(start, size)],
+                    extra_send, extra_recv.at[k - 1], 2 * dest + 1 - quarter % 2, col,
+                )
+                copy.start()
 
     front_loads = [
         pltpu.make_async_copy(front_hbm.at[:, :, h], front_out.at[:, h], front_sem.at[h])
@@ -203,15 +230,22 @@
     for t in range(col_cap):
         found, count = lookup(core, group, t * col_count + col)
         piece = jnp.where(edge < count, diag_ref[found].astype(jnp.float32), 0.0)
-        own_diag[t] = piece.astype(jnp.bfloat16)
+        own_diag[t * block:(t + 1) * block, :] = piece.astype(jnp.bfloat16)
+    swap_copy().start()
+
+    def send_diag():
+        swap_copy().wait_recv()
+        own = own_diag[pl.ds(core * part_rows, part_rows), :].astype(jnp.float32)
+        total = (own + swap_diag[...].astype(jnp.float32)).astype(jnp.bfloat16)
 
         @pl.when(row != diag_row)
         def _():
-            diag_copy(t).start()
+            sum_diag[...] = total
+            diag_copy().start()
 
         @pl.when(row == diag_row)
         def _():
-            diag_in[group, core, t] = own_diag[t]
+            diag_in[group, pl.ds(core * part_rows, part_rows), :] = total
 
     for copy in front_loads:
         copy.start()
@@ -224,11 +258,23 @@
     def add_diag(source):
         for t in range(col_cap):
             b = source * col_cap + t
-            total = diag_in[source, 0, t].astype(jnp.float32) + diag_in[source, 1, t].astype(jnp.float32)
+            total = diag_in[source, t * block:(t + 1) * block, :].astype(jnp.float32)
             spot = pl.ds(b % cols_local, block, stride=cols_local)
             for h in range(block // LANES):
                 held = front_out.at[b * ratio + half, h].reshape(block * cols_local, LANES)
                 held[spot, :] = held[spot, :] + total[:, h * LANES:(h + 1) * LANES]
+
+    def relay_x(count):
+        for i in range(count):
+            for k, source in sources:
+                z_copy(k, source, 1 - par, i).wait_recv()
+                xr_copy(k, source, 1 - par, i).start()
+
+    def relay_z(low, high):
+        for i in range(low, high):
+            for k, source in sources:
+                x_copy(k, source, par, i).wait_recv()
+                zr_copy(k, source, par, i).start()
 
     @pl.when(holder)
     def _():
@@ -237,10 +283,16 @@
                 far_landed(k, source, par, i).wait_recv()
                 x_copy(k, source, par, i).start()
                 z_copy(k, source, par, i).start()
-        for i in range(middle):
-            for k, source in sources:
-                z_copy(k, source, 1 - par, i).wait_recv()
-                xr_copy(k, source, 1 - par, i).start()
+            if i == first:
+                send_diag()
+
+        @pl.when(overlaps(group))
+        def _():
+            relay_x(first)
+
+        @pl.when(jnp.logical_not(overlaps(group)))
+        def _():
+            relay_x(middle)
 
         @pl.when(overlaps(group))
         def _():
@@ -254,10 +306,15 @@
 
     @pl.when(jnp.logical_not(holder))
     def _():
-        for i in range(middle, len(steps)):
-            for k, source in sources:
-                x_copy(k, source, par, i).wait_recv()
-                zr_copy(k, source, par, i).start()
+        send_diag()
+
+        @pl.when(z_over)
+        def _():
+            relay_z(first, middle)
+
+        @pl.when(jnp.logical_not(z_over))
+        def _():
+            relay_z(middle, len(steps))
 
     @pl.when(jnp.logical_not(overlaps(group)))
     def _():
@@ -271,7 +328,7 @@
 
     @pl.when(row == diag_row)
     def _():
-        all_of(diag_in.at[group, 1 - core], diag_send, diag_recv.at[group]).wait_recv()
+        all_of(sum_diag, diag_send, diag_recv.at[group]).wait_recv()
         add_diag(group)
 
     all_of(pair_rows, pair_send, pair_recv).wait_recv()
@@ -281,14 +338,20 @@
     for k, dest in far:
         all_of(far_rows.at[k - 1], far_send.at[k - 1], relay_recv.at[k - 1]).wait_send()
 
+    swap_copy().wait_send()
+
     @pl.when(row != diag_row)
     def _():
-        all_of(own_diag, diag_send, diag_recv.at[group]).wait_send()
+        diag_copy().wait_send()
 
     for k, dest in far:
         @pl.when(jnp.logical_not(overlaps(dest)))
         def _():
             all_of(cols_out.at[group, :, core], col_send.at[k - 1], side_recv.at[k - 1]).wait_send()
+
+        @pl.when(overlaps(dest))
+        def _():
+            all_of(extra_rows, extra_send, extra_recv.at[k - 1]).wait_send()
 
     @pl.when(row == diag_row)
     def _():
@@ -298,6 +361,10 @@
 
     one_part = rows_out.at[group, pl.ds(0, col_cap)]
     half_part = rows_out.at[group, pl.ds(0, col_cap), 0]
+    low_part = extra_rows
+
+    def moved_part(part, k):
+        return all_of(part, relay_send.at[k - 1], relay_recv.at[k - 1])
 
     @pl.when(holder)
     def _():
@@ -306,15 +373,43 @@
                 z_copy(k, source, 1 - par, i).wait_recv()
             all_of(one_part, x_send.at[k - 1], relay_recv.at[k - 1]).wait_send()
             all_of(one_part, z_send.at[k - 1], relay_recv.at[k - 1]).wait_send()
-            all_of(half_part, relay_send.at[k - 1], relay_recv.at[k - 1]).wait_send()
+
+            @pl.when(overlaps(group))
+            def _():
+                for i in range(first, middle):
+                    z_copy(k, source, 1 - par, i).wait_recv()
+                moved_part(low_part, k).wait_send()
+
+            @pl.when(jnp.logical_not(overlaps(group)))
+            def _():
+                moved_part(half_part, k).wait_send()
 
     @pl.when(jnp.logical_not(holder))
     def _():
         for k, source in sources:
-            for i in range(middle):
+            for i in range(first):
                 x_copy(k, source, par, i).wait_recv()
-            all_of(half_part, relay_send.at[k - 1], relay_recv.at[k - 1]).wait_send()
-            all_of(one_part, relay_send.at[k - 1], relay_recv.at[k - 1]).wait_recv()
+
+            @pl.when(z_over)
+            def _():
+                for i in range(middle, len(steps)):
+                    x_copy(k, source, par, i).wait_recv()
+                moved_part(low_part, k).wait_send()
+
+            @pl.when(jnp.logical_not(z_over))
+            def _():
+                for i in range(first, middle):
+                    x_copy(k, source, par, i).wait_recv()
+                moved_part(half_part, k).wait_send()
+
+            @pl.when(overlaps(group))
+            def _():
+                all_of(half_part, extra_send, extra_recv.at[k - 1]).wait_recv()
+                moved_part(half_part, k).wait_recv()
+
+            @pl.when(jnp.logical_not(overlaps(group)))
+            def _():
+                moved_part(one_part, k).wait_recv()
 
     @pl.when(overlaps(group))
     def _():
@@ -385,6 +480,7 @@
         for x in (generators, diagonal_blocks, coupling, block_map, valid_rows, split)
     ]
     far = groups - 1
+    extra = (max(col_cap // 2, 1), block if col_cap > 1 else block // 2, rank)
     rows, cols, front = pl.pallas_call(
         functools.partial(exchange_kernel, row_count, col_count, row_cap, col_cap),
         out_shape=(
@@ -403,14 +499,17 @@
             dma((5,)),
             dma((halves,)),
             pltpu.VMEM((far, col_cap, block, rank), jnp.bfloat16),
+            pltpu.VMEM(extra, jnp.bfloat16),
             pltpu.VMEM((row_cap, block, rank), jnp.bfloat16),
-            pltpu.VMEM((col_cap, block, block), jnp.bfloat16),
-            pltpu.VMEM((groups, 2, col_cap, block, block), jnp.bfloat16),
-            dma((far,)),
-            dma((far, QUAD)),
-            dma((far,)),
-            dma((far,)),
-            dma((far, QUAD)),
+            pltpu.VMEM((col_cap * block, block), jnp.bfloat16),
+            pltpu.VMEM((col_cap * block // 2, block), jnp.bfloat16),
+            pltpu.VMEM((col_cap * block // 2, block), jnp.bfloat16),
+            pltpu.VMEM((groups, col_cap * block, block), jnp.bfloat16),
+            dma((far,)),
+            dma((far, STEPS)),
+            dma((far,)),
+            dma((far,)),
+            dma((far, STEPS)),
             dma((far,)),
             dma((far,)),
             dma,
@@ -422,7 +521,11 @@
             dma((far,)),
             dma((far,)),
             dma,
+            dma,
+            dma,
             dma((groups,)),
+            dma,
+            dma((far,)),
         ],
         compiler_params=pltpu.CompilerParams(
             collective_id=0, has_side_effects=True, vmem_limit_bytes=32 * 1024 * 1024

time: 22.9 us -> 21 us (0.917)
  the two profiles are of different devices: /device:TPU:1 before, /device:TPU:0 now
where the time goes in v4:
time: 21 us; the launch traced here: 20.9 us
  Pallas kernels  20.9 us (100%)
    pallas_call x1, Pallas kernels, shards(): pl.pallas_call(functools.partial(exchange_kernel, row_count, col_count, r...  17.1 us
    pallas_call x1, Pallas kernels, shards(): pl.pallas_call(add_kernel, out_shape=jax.ShapeDtypeStruct(split.shape, jn...  3.73 us

profile of v4, /device:TPU:0, one launch (start us, length us, event | category | flops | bytes accessed | tf_op | source)
XLA Modules:
  0.0 20.9 jit_solution(2948706092754866595)
XLA Ops:
  0.0 17.1 %shard_map.64 = (bf16[2,4,2,256,256]{4,3,2,1,0:T(8,128)(2,1)S(1)}, bf16[2,2,2,256,256]{4,3,2,1,0:T(8,128)(2,1)S(1)}, f32[8,2,256,4,128]{4,3,2,1,0:T(4,128)S(1)}) custom-call(bf16[12,256,256]{2,1,0:T(8,128)(2,1)} %gen_hbm.1, bf16[12,256,256]{2,1,0:T(8,128)(2,1)} %diag_hbm.1, bf16[2,256,256]{2,1,0:T(8,128)(2,1)} %coupling_hbm.1, s32[2,24]{1,0:T(2,128)} %map_hbm.1, ...), custom_call_target="tpu_custom_call" | custom-call | tf_op jit(solution)/shard_map/pallas_call | solution.py:484
  17.1 3.7 %shard_map.65 = f32[8,256,2,4,128]{4,3,2,1,0:T(4,128)} custom-call(f32[8,2,256,4,128]{4,3,2,1,0:T(4,128)S(1)} %get-tuple-element.8.front_ref, bf16[2,4,2,256,256]{4,3,2,1,0:T(8,128)(2,1)S(1)} %get-tuple-element.9.rows_ref, bf16[2,2,2,256,256]{4,3,2,1,0:T(8,128)(2,1)S(1)} %get-tuple-element.10.cols_ref), custom_call_target="tpu_custom_call" | custom-call | tf_op jit(solution)/shard_map/pallas_call | solution.py:534

commit v5 on v4

--- a/solution.py
+++ b/solution.py
@@ -23,7 +23,7 @@
     row_count, col_count, row_cap, col_cap,
     gen_hbm, diag_hbm, coupling_hbm, map_hbm, count_hbm, front_hbm,
     rows_out, cols_out, front_out,
-    gen_ref, diag_ref, coupling_ref, map_ref, count_ref, load_sem, front_sem,
+    gen_ref, near_ref, diag_ref, coupling_ref, map_ref, count_ref, load_sem,
     far_rows, extra_rows, pair_rows, own_diag, swap_diag, sum_diag, diag_in,
     far_send, far_recv, x_send, z_send, step_recv, relay_send, relay_recv,
     pair_send, pair_recv, near_send, near_recv, col_send, col_recv, side_send, side_recv,
@@ -34,12 +34,11 @@
     window = row_cap * row_count
     steps = steps_of(col_cap, block)
     middle = len(steps) // 2
-    first = middle // 2
+    first = len(steps) // 4
+    last = len(steps) // 2
     part_rows = col_cap * block // 2
-    if col_cap == 1:
-        extras = [(0, part_rows, part_rows)]
-    else:
-        extras = [(t, 0, block) for t in range(col_cap // 2, col_cap)]
+    extra_size = col_cap * block // 2
+    extra_t, extra_start, _ = steps[last]
     ratio = col_count // row_count
     cols_local = groups * col_cap
     row = lax.axis_index("row")
@@ -75,10 +74,13 @@
 
     row_iota = lax.broadcasted_iota(jnp.int32, (block, LANES), 0)
 
+    def masked(rows, count):
+        kept = (row_iota < count).astype(jnp.float32).astype(jnp.bfloat16)
+        return rows * jnp.concatenate([kept] * (rank // LANES), axis=1)
+
     def masked_rows(slot):
         found, count = lookup(core, group, slot)
-        kept = (row_iota < count).astype(jnp.float32).astype(jnp.bfloat16)
-        return gen_ref[found] * jnp.concatenate([kept] * (rank // LANES), axis=1)
+        return masked(gen_ref[found], count)
 
     def project(child, rows):
         return lax.dot_general(
@@ -95,14 +97,29 @@
     def load(src, dst, n):
         return pltpu.make_async_copy(src, dst, load_sem.at[n])
 
-    loads = [
-        load(src, dst, n)
-        for n, (src, dst) in enumerate((
-            (map_hbm, map_ref), (count_hbm, count_ref), (gen_hbm, gen_ref),
-            (coupling_hbm, coupling_ref), (diag_hbm, diag_ref),
-        ))
+    far = [(k, (group + k) % groups) for k in range(1, groups)]
+    sources = [(k, (group + groups - k) % groups) for k in range(1, groups)]
+    par = parity(group)
+    spread = near_ref.shape[1]
+
+    def far_slot(dest, t):
+        return (2 * t + parity(dest)) * row_count + 2 * dest + quarter % 2
+
+    def near_start(dest):
+        return jnp.clip(far_slot(dest, 0) - spread + 1, 0, group_blocks - spread)
+
+    map_load = load(map_hbm, map_ref, 0)
+    count_load = load(count_hbm, count_ref, 1)
+    near_loads = [
+        load(gen_hbm.at[pl.ds(near_start(dest), spread)], near_ref.at[k - 1], 2) for k, dest in far
     ]
-    for copy in loads[:4]:
+    gen_load = load(gen_hbm, gen_ref, 3)
+    coupling_load = load(coupling_hbm, coupling_ref, 0)
+    diag_load = load(diag_hbm, diag_ref, 1)
+    front_loads = [
+        load(front_hbm.at[:, :, h], front_out.at[:, h], 2) for h in range(front_out.shape[1])
+    ]
+    for copy in [map_load, count_load] + near_loads:
         copy.start()
 
     barrier = pltpu.get_barrier_semaphore()
@@ -153,18 +170,17 @@
         piece = cols_out.at[group, t, child]
         return remote(piece, piece, near_send, near_recv, pair_row, col)
 
-    def col_copy(k, source, t, dest):
-        piece = cols_out.at[source, t, core]
+    def col_part(source, t, p):
+        return cols_out.at[source, t, :, pl.ds(p * rank // 2, rank // 2)]
+
+    def col_copy(k, t, p, dest):
+        piece = cols_out.at[group, t, core, pl.ds(p * rank // 2, rank // 2)]
         return remote(
-            piece, piece, col_send.at[k - 1], col_recv.at[k - 1, t], 2 * dest + core, col
-        )
-
-    def fwd_copy(k, source, t):
-        piece = cols_out.at[source, t, core]
-        return remote(piece, piece, side_send.at[k - 1], side_recv.at[k - 1], pair_row, col)
-
-    def over_copy(k, source, t):
-        piece = cols_out.at[source, t]
+            piece, piece, col_send.at[k - 1], col_recv.at[k - 1, 2 * t + p], 2 * dest + 1, col
+        )
+
+    def side_copy(k, source, t, p):
+        piece = col_part(source, t, p)
         return remote(piece, piece, side_send.at[k - 1], side_recv.at[k - 1], pair_row, col)
 
     def swap_copy():
@@ -179,51 +195,53 @@
             diag_send, diag_recv.at[group], diag_row, col,
         )
 
-    far = [(k, (group + k) % groups) for k in range(1, groups)]
-    sources = [(k, (group + groups - k) % groups) for k in range(1, groups)]
-    par = parity(group)
-
-    for copy in loads[:3]:
-        copy.wait()
-    loads[4].start()
+    map_load.wait()
+    count_load.wait()
+    gen_load.start()
+    coupling_load.start()
+    diag_load.start()
+    load(near_ref, near_ref, 2).wait()
     for t in range(col_cap):
         for k, dest in far:
-            slot = (2 * t + parity(dest)) * row_count + 2 * dest + quarter % 2
-            far_rows[k - 1, t] = masked_rows(slot)
+            if t == 0:
+                found, count = lookup(core, group, far_slot(dest, 0))
+                at = jnp.maximum(found - near_start(dest), 0)
+                far_rows[k - 1, 0] = masked(near_ref[k - 1, at], count)
+            else:
+                far_rows[k - 1, t] = masked_rows(far_slot(dest, t))
         if t == 0:
             pl.semaphore_wait(barrier, row_count + 1)
         for i in range(len(steps)):
             if steps[i][0] == t:
                 for k, dest in far:
                     far_copy(k, core, group, parity(dest), i, 2 * dest + quarter % 2).start()
+        if t == 0:
+            gen_load.wait()
     for k, dest in far:
         @pl.when(overlaps(dest))
         def _():
-            for n, (t, start, size) in enumerate(extras):
-                slot = (2 * t + 1 - parity(dest)) * row_count + 2 * dest + 1 - quarter % 2
-                extra_rows[n] = masked_rows(slot)[start:start + size]
-                copy = remote(
-                    extra_rows.at[n],
-                    rows_out.at[group, 2 * t + 1 - parity(dest), core, pl.ds(start, size)],
-                    extra_send, extra_recv.at[k - 1], 2 * dest + 1 - quarter % 2, col,
-                )
-                copy.start()
-
-    front_loads = [
-        pltpu.make_async_copy(front_hbm.at[:, :, h], front_out.at[:, h], front_sem.at[h])
-        for h in range(front_out.shape[1])
-    ]
-    for copy in loads[3:]:
-        copy.wait()
-
+            slot_row = 2 * extra_t + 1 - parity(dest)
+            slot = slot_row * row_count + 2 * dest + 1 - quarter % 2
+            extra_rows[...] = masked_rows(slot)[extra_start:extra_start + extra_size]
+            copy = remote(
+                extra_rows, rows_out.at[group, slot_row, core, pl.ds(extra_start, extra_size)],
+                extra_send, extra_recv.at[k - 1], 2 * dest + 1 - quarter % 2, col,
+            )
+            copy.start()
+
+    coupling_load.wait()
     for t in range(col_cap):
         cols_out[group, t, core] = project(core, masked_rows(t * col_count + col))
         near_copy(core, t).start()
         for k, dest in far:
             @pl.when(jnp.logical_not(overlaps(dest)))
             def _():
-                col_copy(k, group, t, dest).start()
-
+                for p in range(2):
+                    col_copy(k, t, p, dest).start()
+
+    diag_load.wait()
+    for copy in front_loads:
+        copy.start()
     row_iota2 = lax.broadcasted_iota(jnp.int32, (block, block), 0)
     col_iota2 = lax.broadcasted_iota(jnp.int32, (block, block), 1)
     edge = jnp.maximum(row_iota2, col_iota2)
@@ -247,13 +265,14 @@
         def _():
             diag_in[group, pl.ds(core * part_rows, part_rows), :] = total
 
-    for copy in front_loads:
-        copy.start()
-    for m in range(row_cap):
-        pair_rows[m] = masked_rows(m * row_count + pair_row)
-        pair_copy(core, m).start()
-    for m in range(row_cap):
-        rows_out[group, m, core] = masked_rows(m * row_count + row)
+    def send_pair():
+        for m in range(row_cap):
+            pair_rows[m] = masked_rows(m * row_count + pair_row)
+            pair_copy(core, m).start()
+
+    def keep_own():
+        for m in range(row_cap):
+            rows_out[group, m, core] = masked_rows(m * row_count + row)
 
     def add_diag(source):
         for t in range(col_cap):
@@ -283,8 +302,12 @@
                 far_landed(k, source, par, i).wait_recv()
                 x_copy(k, source, par, i).start()
                 z_copy(k, source, par, i).start()
-            if i == first:
+            if i == 1:
+                send_pair()
+            if i == middle // 2:
                 send_diag()
+            if i == middle:
+                keep_own()
 
         @pl.when(overlaps(group))
         def _():
@@ -302,29 +325,33 @@
                         cols_out[source, t, child] = project(
                             child, rows_out[source, 2 * t + par, child]
                         )
-                    over_copy(k, source, t).start()
+                    for p in range(2):
+                        side_copy(k, source, t, p).start()
 
     @pl.when(jnp.logical_not(holder))
     def _():
+        send_pair()
+        keep_own()
         send_diag()
 
         @pl.when(z_over)
         def _():
-            relay_z(first, middle)
+            relay_z(first, last)
 
         @pl.when(jnp.logical_not(z_over))
         def _():
             relay_z(middle, len(steps))
 
-    @pl.when(jnp.logical_not(overlaps(group)))
+    @pl.when(jnp.logical_and(jnp.logical_not(overlaps(group)), core == 1))
     def _():
         for t in range(col_cap):
-            for k, source in sources:
-                col_copy(k, source, t, group).wait_recv()
-                fwd_copy(k, source, t).start()
-
-    for copy in front_loads:
-        copy.wait()
+            for p in range(2):
+                for k, source in sources:
+                    both = col_part(source, t, p)
+                    all_of(both, col_send.at[k - 1], col_recv.at[k - 1, 2 * t + p]).wait_recv()
+                    side_copy(k, source, t, p).start()
+
+    load(front_out, front_out, 2).wait()
 
     @pl.when(row == diag_row)
     def _():
@@ -361,10 +388,10 @@
 
     one_part = rows_out.at[group, pl.ds(0, col_cap)]
     half_part = rows_out.at[group, pl.ds(0, col_cap), 0]
-    low_part = extra_rows
-
-    def moved_part(part, k):
-        return all_of(part, relay_send.at[k - 1], relay_recv.at[k - 1])
+
+    low_part = rows_out.at[group, 0, :, pl.ds(0, part_rows // 2)]
+    part_of_extra = rows_out.at[group, 0, :, pl.ds(0, extra_size)]
+    over_part = rows_out.at[group, pl.ds(0, 2), :, pl.ds(0, part_rows // 2)]
 
     @pl.when(holder)
     def _():
@@ -378,11 +405,11 @@
             def _():
                 for i in range(first, middle):
                     z_copy(k, source, 1 - par, i).wait_recv()
-                moved_part(low_part, k).wait_send()
+                all_of(low_part, relay_send.at[k - 1], relay_recv.at[k - 1]).wait_send()
 
             @pl.when(jnp.logical_not(overlaps(group)))
             def _():
-                moved_part(half_part, k).wait_send()
+                all_of(half_part, relay_send.at[k - 1], relay_recv.at[k - 1]).wait_send()
 
     @pl.when(jnp.logical_not(holder))
     def _():
@@ -392,44 +419,36 @@
 
             @pl.when(z_over)
             def _():
-                for i in range(middle, len(steps)):
+                for i in range(last, len(steps)):
                     x_copy(k, source, par, i).wait_recv()
-                moved_part(low_part, k).wait_send()
+                all_of(low_part, relay_send.at[k - 1], relay_recv.at[k - 1]).wait_send()
 
             @pl.when(jnp.logical_not(z_over))
             def _():
                 for i in range(first, middle):
                     x_copy(k, source, par, i).wait_recv()
-                moved_part(half_part, k).wait_send()
+                all_of(half_part, relay_send.at[k - 1], relay_recv.at[k - 1]).wait_send()
 
             @pl.when(overlaps(group))
             def _():
-                all_of(half_part, extra_send, extra_recv.at[k - 1]).wait_recv()
-                moved_part(half_part, k).wait_recv()
+                all_of(part_of_extra, extra_send, extra_recv.at[k - 1]).wait_recv()
+                all_of(over_part, relay_send.at[k - 1], relay_recv.at[k - 1]).wait_recv()
 
             @pl.when(jnp.logical_not(overlaps(group)))
             def _():
-                moved_part(one_part, k).wait_recv()
-
-    @pl.when(overlaps(group))
-    def _():
-        for k, source in sources:
-            moved = all_of(cols_out.at[source], side_send.at[k - 1], side_recv.at[k - 1])
-
-            @pl.when(holder)
-            def _():
-                moved.wait_send()
-
-            @pl.when(jnp.logical_not(holder))
-            def _():
-                moved.wait_recv()
-
-    @pl.when(jnp.logical_not(overlaps(group)))
-    def _():
-        for k, source in sources:
-            moved = all_of(cols_out.at[source, :, core], side_send.at[k - 1], side_recv.at[k - 1])
-            moved.wait_recv()
-            moved.wait_send()
+                all_of(one_part, relay_send.at[k - 1], relay_recv.at[k - 1]).wait_recv()
+
+    gives = jnp.where(overlaps(group), holder, core == 1)
+    for k, source in sources:
+        side = all_of(cols_out.at[source], side_send.at[k - 1], side_recv.at[k - 1])
+
+        @pl.when(gives)
+        def _():
+            side.wait_send()
+
+        @pl.when(jnp.logical_not(gives))
+        def _():
+            side.wait_recv()
 
 
 def add_kernel(
@@ -439,23 +458,26 @@
     _, row_cap, _, _, rank = rows_ref.shape
     col_cap = cols_ref.shape[1]
 
-    def write(a, h):
-        return pltpu.make_async_copy(staged.at[a, h], out_ref.at[a, :, h], out_sem)
-
     for a in range(rows_local):
         s, m = divmod(a, row_cap)
-        rows = jnp.concatenate([rows_ref[s, m, 0], rows_ref[s, m, 1]], axis=1)
-        for b in range(cols_local):
-            cols = cols_ref[b // col_cap, b % col_cap].reshape(2 * rank, block)
-            tile = jnp.dot(rows, cols, preferred_element_type=jnp.float32)
-            spot = pl.ds(b, block, stride=cols_local)
+        cuts = (0, block // 2, block) if a < 2 else (0, block)
+        for low, high in zip(cuts[:-1], cuts[1:]):
+            size = high - low
+            rows = jnp.concatenate(
+                [rows_ref[s, m, 0, low:high], rows_ref[s, m, 1, low:high]], axis=1
+            )
+            for b in range(cols_local):
+                cols = cols_ref[b // col_cap, b % col_cap].reshape(2 * rank, block)
+                tile = jnp.dot(rows, cols, preferred_element_type=jnp.float32)
+                spot = pl.ds(low * cols_local + b, size, stride=cols_local)
+                for h in range(halves):
+                    src = front_ref.at[a, h].reshape(block * cols_local, LANES)
+                    dst = staged.at[a, h].reshape(block * cols_local, LANES)
+                    dst[spot, :] = src[spot, :] + tile[:, h * LANES:(h + 1) * LANES]
             for h in range(halves):
-                src = front_ref.at[a, h].reshape(block * cols_local, LANES)
-                dst = staged.at[a, h].reshape(block * cols_local, LANES)
-                dst[spot, :] = src[spot, :] + tile[:, h * LANES:(h + 1) * LANES]
-
-        for h in range(halves):
-            write(a, h).start()
+                pltpu.make_async_copy(
+                    staged.at[a, h, low:high], out_ref.at[a, low:high, h], out_sem
+                ).start()
     pltpu.make_async_copy(staged, staged, out_sem).wait()
 
 
@@ -480,7 +502,9 @@
         for x in (generators, diagonal_blocks, coupling, block_map, valid_rows, split)
     ]
     far = groups - 1
-    extra = (max(col_cap // 2, 1), block if col_cap > 1 else block // 2, rank)
+    group_blocks = generators.shape[0]
+    near = (far, row_cap * row_count - group_blocks + 1, block, rank)
+    extra = (col_cap * block // 2, rank)
     rows, cols, front = pl.pallas_call(
         functools.partial(exchange_kernel, row_count, col_count, row_cap, col_cap),
         out_shape=(
@@ -492,12 +516,12 @@
         out_specs=(vmem,) * 3,
         scratch_shapes=[
             pltpu.VMEM(generators.shape, jnp.bfloat16),
+            pltpu.VMEM(near, jnp.bfloat16),
             pltpu.VMEM(diagonal_blocks.shape, jnp.bfloat16),
             pltpu.VMEM(coupling.shape, jnp.bfloat16),
             pltpu.SMEM(block_map.shape, jnp.int32),
             pltpu.SMEM(valid_rows.shape, jnp.int32),
-            dma((5,)),
-            dma((halves,)),
+            dma((4,)),
             pltpu.VMEM((far, col_cap, block, rank), jnp.bfloat16),
             pltpu.VMEM(extra, jnp.bfloat16),
             pltpu.VMEM((row_cap, block, rank), jnp.bfloat16),
@@ -517,7 +541,7 @@
             dma,
             dma,
             dma((far,)),
-            dma((far, col_cap)),
+            dma((far, 2 * col_cap)),
             dma((far,)),
             dma((far,)),
             dma,

time: 21 us -> 20.9 us (level)
  no operation moved by 1% of the time
where the time goes in v5:
time: 20.9 us; the launch traced here: 20.7 us
  Pallas kernels  20.7 us (99%)
    pallas_call x1, Pallas kernels, shards(): pl.pallas_call(functools.partial(exchange_kernel, row_count, col_count, r...  17.1 us
    pallas_call x1, Pallas kernels, shards(): pl.pallas_call(add_kernel, out_shape=jax.ShapeDtypeStruct(split.shape, jn...  3.6 us

profile of v5, /device:TPU:0, one launch (start us, length us, event | category | flops | bytes accessed | tf_op | source)
XLA Modules:
  0.0 20.7 jit_solution(4782319969468249168)
XLA Ops:
  0.0 17.1 %shard_map.64 = (bf16[2,4,2,256,256]{4,3,2,1,0:T(8,128)(2,1)S(1)}, bf16[2,2,2,256,256]{4,3,2,1,0:T(8,128)(2,1)S(1)}, f32[8,2,256,4,128]{4,3,2,1,0:T(4,128)S(1)}) custom-call(bf16[12,256,256]{2,1,0:T(8,128)(2,1)} %gen_hbm.1, bf16[12,256,256]{2,1,0:T(8,128)(2,1)} %diag_hbm.1, bf16[2,256,256]{2,1,0:T(8,128)(2,1)} %coupling_hbm.1, s32[2,24]{1,0:T(2,128)} %map_hbm.1, ...), custom_call_target="tpu_custom_call" | custom-call | tf_op jit(solution)/shard_map/pallas_call | solution.py:508
  17.1 3.6 %shard_map.65 = f32[8,256,2,4,128]{4,3,2,1,0:T(4,128)} custom-call(f32[8,2,256,4,128]{4,3,2,1,0:T(4,128)S(1)} %get-tuple-element.8.front_ref, bf16[2,4,2,256,256]{4,3,2,1,0:T(8,128)(2,1)S(1)} %get-tuple-element.9.rows_ref, bf16[2,2,2,256,256]{4,3,2,1,0:T(8,128)(2,1)S(1)} %get-tuple-element.10.cols_ref), custom_call_target="tpu_custom_call" | custom-call | tf_op jit(solution)/shard_map/pallas_call | solution.py:558

commit v6 on v5

--- a/solution.py
+++ b/solution.py
@@ -25,7 +25,7 @@
     rows_out, cols_out, front_out,
     gen_ref, near_ref, diag_ref, coupling_ref, map_ref, count_ref, load_sem,
     far_rows, extra_rows, pair_rows, own_diag, swap_diag, sum_diag, diag_in,
-    far_send, far_recv, x_send, z_send, step_recv, relay_send, relay_recv,
+    far_send, far_recv, both_send, z_recv, relay_send, relay_recv,
     pair_send, pair_recv, near_send, near_recv, col_send, col_recv, side_send, side_recv,
     swap_send, swap_recv, diag_send, diag_recv, extra_send, extra_recv,
 ):
@@ -34,10 +34,11 @@
     window = row_cap * row_count
     steps = steps_of(col_cap, block)
     middle = len(steps) // 2
-    first = len(steps) // 4
-    last = len(steps) // 2
+    first = middle - 2
+    last = middle + 1
+    step_rows = steps[0][2]
     part_rows = col_cap * block // 2
-    extra_size = col_cap * block // 2
+    extra_size = (len(steps) - last) * step_rows
     extra_t, extra_start, _ = steps[last]
     ratio = col_count // row_count
     cols_local = groups * col_cap
@@ -147,16 +148,16 @@
         return piece_copy(source, par, i, far_send.at[k - 1], far_recv.at[k - 1, i], col)
 
     def x_copy(k, source, par, i):
-        return piece_copy(source, par, i, x_send.at[k - 1], step_recv.at[k - 1, i], x_col)
+        return piece_copy(source, par, i, both_send.at[k - 1], far_recv.at[k - 1, i], x_col)
 
     def z_copy(k, source, par, i):
-        return piece_copy(source, par, i, z_send.at[k - 1], step_recv.at[k - 1, i], z_col)
+        return piece_copy(source, par, i, both_send.at[k - 1], z_recv.at[k - 1, min(i, middle)], z_col)
 
     def xr_copy(k, source, par, i):
-        return piece_copy(source, par, i, relay_send.at[k - 1], relay_recv.at[k - 1], x_col)
+        return piece_copy(source, par, i, relay_send.at[k - 1], relay_recv.at[k - 1, 0], x_col)
 
     def zr_copy(k, source, par, i):
-        return piece_copy(source, par, i, relay_send.at[k - 1], relay_recv.at[k - 1], z_col)
+        return piece_copy(source, par, i, relay_send.at[k - 1], relay_recv.at[k - 1, 1], z_col)
 
     def all_of(ref, send, recv):
         return remote(ref, ref, send, recv, pair_row, col)
@@ -363,7 +364,7 @@
     all_of(cols_out.at[group, :, 1 - core], near_send, near_recv).wait_recv()
     all_of(cols_out.at[group, :, core], near_send, near_recv).wait_send()
     for k, dest in far:
-        all_of(far_rows.at[k - 1], far_send.at[k - 1], relay_recv.at[k - 1]).wait_send()
+        all_of(far_rows.at[k - 1], far_send.at[k - 1], relay_recv.at[k - 1, 0]).wait_send()
 
     swap_copy().wait_send()
 
@@ -386,30 +387,29 @@
             all_of(diag_in.at[source], diag_send, diag_recv.at[source]).wait_recv()
             add_diag(source)
 
-    one_part = rows_out.at[group, pl.ds(0, col_cap)]
-    half_part = rows_out.at[group, pl.ds(0, col_cap), 0]
-
-    low_part = rows_out.at[group, 0, :, pl.ds(0, part_rows // 2)]
-    part_of_extra = rows_out.at[group, 0, :, pl.ds(0, extra_size)]
-    over_part = rows_out.at[group, pl.ds(0, 2), :, pl.ds(0, part_rows // 2)]
+    def rows_of(count):
+        return rows_out.at[group, 0, :, pl.ds(0, count * step_rows)]
+
+    def relayed(k, count, way):
+        return all_of(rows_of(count), relay_send.at[k - 1], relay_recv.at[k - 1, way])
+
+    rest = len(steps) - middle
 
     @pl.when(holder)
     def _():
         for k, source in sources:
-            for i in range(middle, len(steps)):
-                z_copy(k, source, 1 - par, i).wait_recv()
-            all_of(one_part, x_send.at[k - 1], relay_recv.at[k - 1]).wait_send()
-            all_of(one_part, z_send.at[k - 1], relay_recv.at[k - 1]).wait_send()
+            all_of(rows_of(rest), both_send.at[k - 1], z_recv.at[k - 1, middle]).wait_recv()
+            all_of(rows_out.at[group], both_send.at[k - 1], z_recv.at[k - 1, 0]).wait_send()
 
             @pl.when(overlaps(group))
             def _():
                 for i in range(first, middle):
                     z_copy(k, source, 1 - par, i).wait_recv()
-                all_of(low_part, relay_send.at[k - 1], relay_recv.at[k - 1]).wait_send()
+                relayed(k, first, 0).wait_send()
 
             @pl.when(jnp.logical_not(overlaps(group)))
             def _():
-                all_of(half_part, relay_send.at[k - 1], relay_recv.at[k - 1]).wait_send()
+                relayed(k, middle, 0).wait_send()
 
     @pl.when(jnp.logical_not(holder))
     def _():
@@ -421,22 +421,24 @@
             def _():
                 for i in range(last, len(steps)):
                     x_copy(k, source, par, i).wait_recv()
-                all_of(low_part, relay_send.at[k - 1], relay_recv.at[k - 1]).wait_send()
+                relayed(k, last - first, 0).wait_send()
 
             @pl.when(jnp.logical_not(z_over))
             def _():
                 for i in range(first, middle):
                     x_copy(k, source, par, i).wait_recv()
-                all_of(half_part, relay_send.at[k - 1], relay_recv.at[k - 1]).wait_send()
+                relayed(k, rest, 0).wait_send()
 
             @pl.when(overlaps(group))
             def _():
-                all_of(part_of_extra, extra_send, extra_recv.at[k - 1]).wait_recv()
-                all_of(over_part, relay_send.at[k - 1], relay_recv.at[k - 1]).wait_recv()
+                all_of(rows_of(len(steps) - last), extra_send, extra_recv.at[k - 1]).wait_recv()
+                relayed(k, first, 0).wait_recv()
+                relayed(k, last - first, 1).wait_recv()
 
             @pl.when(jnp.logical_not(overlaps(group)))
             def _():
-                all_of(one_part, relay_send.at[k - 1], relay_recv.at[k - 1]).wait_recv()
+                relayed(k, middle, 0).wait_recv()
+                relayed(k, rest, 1).wait_recv()
 
     gives = jnp.where(overlaps(group), holder, core == 1)
     for k, source in sources:
@@ -504,7 +506,7 @@
     far = groups - 1
     group_blocks = generators.shape[0]
     near = (far, row_cap * row_count - group_blocks + 1, block, rank)
-    extra = (col_cap * block // 2, rank)
+    extra = (col_cap * block * (STEPS // 2 - 1) // STEPS, rank)
     rows, cols, front = pl.pallas_call(
         functools.partial(exchange_kernel, row_count, col_count, row_cap, col_cap),
         out_shape=(
@@ -532,10 +534,9 @@
             dma((far,)),
             dma((far, STEPS)),
             dma((far,)),
-            dma((far,)),
-            dma((far, STEPS)),
-            dma((far,)),
-            dma((far,)),
+            dma((far, STEPS // 2 + 1)),
+            dma((far,)),
+            dma((far, 2)),
             dma,
             dma,
             dma,

time: 20.9 us -> 20.5 us (0.981)
  Pallas kernels: 20.7 us -> 20.3 us
    pallas_call x1, Pallas kernels: 17.1 us -> 16.7 us  [shards(): pl.pallas_call(functools.partial(exchange_kernel, row_count, col_count, r...]
where the time goes in v6:
time: 20.5 us; the launch traced here: 20.3 us
  Pallas kernels  20.3 us (99%)
    pallas_call x1, Pallas kernels, shards(): pl.pallas_call(functools.partial(exchange_kernel, row_count, col_count, r...  16.7 us
    pallas_call x1, Pallas kernels, shards(): pl.pallas_call(add_kernel, out_shape=jax.ShapeDtypeStruct(split.shape, jn...  3.61 us

profile of v6, /device:TPU:0, one launch (start us, length us, event | category | flops | bytes accessed | tf_op | source)
XLA Modules:
  0.0 20.3 jit_solution(1744029173378280895)
XLA Ops:
  0.0 16.7 %shard_map.64 = (bf16[2,4,2,256,256]{4,3,2,1,0:T(8,128)(2,1)S(1)}, bf16[2,2,2,256,256]{4,3,2,1,0:T(8,128)(2,1)S(1)}, f32[8,2,256,4,128]{4,3,2,1,0:T(4,128)S(1)}) custom-call(bf16[12,256,256]{2,1,0:T(8,128)(2,1)} %gen_hbm.1, bf16[12,256,256]{2,1,0:T(8,128)(2,1)} %diag_hbm.1, bf16[2,256,256]{2,1,0:T(8,128)(2,1)} %coupling_hbm.1, s32[2,24]{1,0:T(2,128)} %map_hbm.1, ...), custom_call_target="tpu_custom_call" | custom-call | tf_op jit(solution)/shard_map/pallas_call | solution.py:510
  16.7 3.6 %shard_map.65 = f32[8,256,2,4,128]{4,3,2,1,0:T(4,128)} custom-call(f32[8,2,256,4,128]{4,3,2,1,0:T(4,128)S(1)} %get-tuple-element.8.front_ref, bf16[2,4,2,256,256]{4,3,2,1,0:T(8,128)(2,1)S(1)} %get-tuple-element.9.rows_ref, bf16[2,2,2,256,256]{4,3,2,1,0:T(8,128)(2,1)S(1)} %get-tuple-element.10.cols_ref), custom_call_target="tpu_custom_call" | custom-call | tf_op jit(solution)/shard_map/pallas_call | solution.py:559

commit v7 on v6

--- a/solution.py
+++ b/solution.py
@@ -9,14 +9,22 @@
 
 MESH = pl.DeviceIdType.MESH
 QUAD = 4
-STEPS = 16
+UNITS = 16
+SIZES = (1, 1, 1, 1, 1, 1, 1, 1, 1, 1, 1, 1, 1, 1, 1, 1)
+HALF_AT = 8
+FIRST_AT = 6
+LAST_AT = 9
 LANES = 128
 
 
 def steps_of(col_cap, block):
-    per_block = STEPS // col_cap
-    size = block // per_block
-    return [(t, p * size, size) for t in range(col_cap) for p in range(per_block)]
+    unit = col_cap * block // UNITS
+    steps = []
+    start = 0
+    for size in SIZES:
+        steps.append((start // block, start % block, size * unit))
+        start += size * unit
+    return steps
 
 
 def exchange_kernel(
@@ -33,12 +41,11 @@
     group_blocks, block, rank = gen_ref.shape
     window = row_cap * row_count
     steps = steps_of(col_cap, block)
-    middle = len(steps) // 2
-    first = middle - 2
-    last = middle + 1
-    step_rows = steps[0][2]
+    middle = HALF_AT
+    first = FIRST_AT
+    last = LAST_AT
     part_rows = col_cap * block // 2
-    extra_size = (len(steps) - last) * step_rows
+    extra_size = sum(size for _, _, size in steps[last:])
     extra_t, extra_start, _ = steps[last]
     ratio = col_count // row_count
     cols_local = groups * col_cap
@@ -98,6 +105,14 @@
     def load(src, dst, n):
         return pltpu.make_async_copy(src, dst, load_sem.at[n])
 
+    barrier = pltpu.get_barrier_semaphore()
+    for k in range(1, row_count):
+        pl.semaphore_signal(
+            barrier, inc=1, device_id=((row + k) % row_count, col), device_id_type=MESH
+        )
+    for other in (x_col, z_col):
+        pl.semaphore_signal(barrier, inc=1, device_id=(row, other), device_id_type=MESH)
+
     far = [(k, (group + k) % groups) for k in range(1, groups)]
     sources = [(k, (group + groups - k) % groups) for k in range(1, groups)]
     par = parity(group)
@@ -123,14 +138,6 @@
     for copy in [map_load, count_load] + near_loads:
         copy.start()
 
-    barrier = pltpu.get_barrier_semaphore()
-    for k in range(1, row_count):
-        pl.semaphore_signal(
-            barrier, inc=1, device_id=((row + k) % row_count, col), device_id_type=MESH
-        )
-    for other in (x_col, z_col):
-        pl.semaphore_signal(barrier, inc=1, device_id=(row, other), device_id_type=MESH)
-
     def far_copy(k, child, source, par, i, dest_row):
         t, start, size = steps[i]
         part = pl.ds(start, size)
@@ -172,10 +179,10 @@
         return remote(piece, piece, near_send, near_recv, pair_row, col)
 
     def col_part(source, t, p):
-        return cols_out.at[source, t, :, pl.ds(p * rank // 2, rank // 2)]
+        return cols_out.at[source, t, :, pl.ds(p * rank * 3 // 4, rank * (3 - 2 * p) // 4)]
 
     def col_copy(k, t, p, dest):
-        piece = cols_out.at[group, t, core, pl.ds(p * rank // 2, rank // 2)]
+        piece = cols_out.at[group, t, core, pl.ds(p * rank * 3 // 4, rank * (3 - 2 * p) // 4)]
         return remote(
             piece, piece, col_send.at[k - 1], col_recv.at[k - 1, 2 * t + p], 2 * dest + 1, col
         )
@@ -387,29 +394,29 @@
             all_of(diag_in.at[source], diag_send, diag_recv.at[source]).wait_recv()
             add_diag(source)
 
-    def rows_of(count):
-        return rows_out.at[group, 0, :, pl.ds(0, count * step_rows)]
-
-    def relayed(k, count, way):
-        return all_of(rows_of(count), relay_send.at[k - 1], relay_recv.at[k - 1, way])
-
-    rest = len(steps) - middle
+    end = len(steps)
+
+    def rows_of(low, high):
+        return rows_out.at[group, 0, :, pl.ds(0, sum(size for _, _, size in steps[low:high]))]
+
+    def relayed(k, low, high, way):
+        return all_of(rows_of(low, high), relay_send.at[k - 1], relay_recv.at[k - 1, way])
 
     @pl.when(holder)
     def _():
         for k, source in sources:
-            all_of(rows_of(rest), both_send.at[k - 1], z_recv.at[k - 1, middle]).wait_recv()
+            all_of(rows_of(middle, end), both_send.at[k - 1], z_recv.at[k - 1, middle]).wait_recv()
             all_of(rows_out.at[group], both_send.at[k - 1], z_recv.at[k - 1, 0]).wait_send()
 
             @pl.when(overlaps(group))
             def _():
                 for i in range(first, middle):
                     z_copy(k, source, 1 - par, i).wait_recv()
-                relayed(k, first, 0).wait_send()
+                relayed(k, 0, first, 0).wait_send()
 
             @pl.when(jnp.logical_not(overlaps(group)))
             def _():
-                relayed(k, middle, 0).wait_send()
+                relayed(k, 0, middle, 0).wait_send()
 
     @pl.when(jnp.logical_not(holder))
     def _():
@@ -421,24 +428,24 @@
             def _():
                 for i in range(last, len(steps)):
                     x_copy(k, source, par, i).wait_recv()
-                relayed(k, last - first, 0).wait_send()
+                relayed(k, first, last, 0).wait_send()
 
             @pl.when(jnp.logical_not(z_over))
             def _():
                 for i in range(first, middle):
                     x_copy(k, source, par, i).wait_recv()
-                relayed(k, rest, 0).wait_send()
+                relayed(k, middle, end, 0).wait_send()
 
             @pl.when(overlaps(group))
             def _():
-                all_of(rows_of(len(steps) - last), extra_send, extra_recv.at[k - 1]).wait_recv()
-                relayed(k, first, 0).wait_recv()
-                relayed(k, last - first, 1).wait_recv()
+                all_of(rows_of(last, end), extra_send, extra_recv.at[k - 1]).wait_recv()
+                relayed(k, 0, first, 0).wait_recv()
+                relayed(k, first, last, 1).wait_recv()
 
             @pl.when(jnp.logical_not(overlaps(group)))
             def _():
-                relayed(k, middle, 0).wait_recv()
-                relayed(k, rest, 1).wait_recv()
+                relayed(k, 0, middle, 0).wait_recv()
+                relayed(k, middle, end, 1).wait_recv()
 
     gives = jnp.where(overlaps(group), holder, core == 1)
     for k, source in sources:
@@ -462,7 +469,7 @@
 
     for a in range(rows_local):
         s, m = divmod(a, row_cap)
-        cuts = (0, block // 2, block) if a < 2 else (0, block)
+        cuts = (0, block // 2, block) if a < 4 else (0, block)
         for low, high in zip(cuts[:-1], cuts[1:]):
             size = high - low
             rows = jnp.concatenate(
@@ -506,7 +513,7 @@
     far = groups - 1
     group_blocks = generators.shape[0]
     near = (far, row_cap * row_count - group_blocks + 1, block, rank)
-    extra = (col_cap * block * (STEPS // 2 - 1) // STEPS, rank)
+    extra = (col_cap * block * sum(SIZES[LAST_AT:]) // UNITS, rank)
     rows, cols, front = pl.pallas_call(
         functools.partial(exchange_kernel, row_count, col_count, row_cap, col_cap),
         out_shape=(
@@ -532,9 +539,9 @@
             pltpu.VMEM((col_cap * block // 2, block), jnp.bfloat16),
             pltpu.VMEM((groups, col_cap * block, block), jnp.bfloat16),
             dma((far,)),
-            dma((far, STEPS)),
-            dma((far,)),
-            dma((far, STEPS // 2 + 1)),
+            dma((far, len(SIZES))),
+            dma((far,)),
+            dma((far, HALF_AT + 1)),
             dma((far,)),
             dma((far, 2)),
             dma,

time: 20.5 us -> 20.5 us (level)
  no operation moved by 1% of the time
where the time goes in v7:
time: 20.5 us; the launch traced here: 20.3 us
  Pallas kernels  20.3 us (99%)
    pallas_call x1, Pallas kernels, shards(): pl.pallas_call(functools.partial(exchange_kernel, row_count, col_count, r...  16.7 us
    pallas_call x1, Pallas kernels, shards(): pl.pallas_call(add_kernel, out_shape=jax.ShapeDtypeStruct(split.shape, jn...  3.59 us

profile of v7, /device:TPU:0, one launch (start us, length us, event | category | flops | bytes accessed | tf_op | source)
XLA Modules:
  0.0 20.3 jit_solution(17439522598199908607)
XLA Ops:
  0.0 16.7 %shard_map.64 = (bf16[2,4,2,256,256]{4,3,2,1,0:T(8,128)(2,1)S(1)}, bf16[2,2,2,256,256]{4,3,2,1,0:T(8,128)(2,1)S(1)}, f32[8,2,256,4,128]{4,3,2,1,0:T(4,128)S(1)}) custom-call(bf16[12,256,256]{2,1,0:T(8,128)(2,1)} %gen_hbm.1, bf16[12,256,256]{2,1,0:T(8,128)(2,1)} %diag_hbm.1, bf16[2,256,256]{2,1,0:T(8,128)(2,1)} %coupling_hbm.1, s32[2,24]{1,0:T(2,128)} %map_hbm.1, ...), custom_call_target="tpu_custom_call" | custom-call | tf_op jit(solution)/shard_map/pallas_call | solution.py:517
  16.7 3.6 %shard_map.65 = f32[8,256,2,4,128]{4,3,2,1,0:T(4,128)} custom-call(f32[8,2,256,4,128]{4,3,2,1,0:T(4,128)S(1)} %get-tuple-element.8.front_ref, bf16[2,4,2,256,256]{4,3,2,1,0:T(8,128)(2,1)S(1)} %get-tuple-element.9.rows_ref, bf16[2,2,2,256,256]{4,3,2,1,0:T(8,128)(2,1)S(1)} %get-tuple-element.10.cols_ref), custom_call_target="tpu_custom_call" | custom-call | tf_op jit(solution)/shard_map/pallas_call | solution.py:566
